TPU v7x, 512 devices: a whole 4x4x16 slice. The times are simulated.
512 devices in a mesh: rows: 128 (over x, z_lo, y), cols: 4 (over z_hi, core).
Axes of the slice: x: 4, y: 4, z: 16 (z_hi: 2, z_lo: 8; z = z_hi * 8 + z_lo), core: 2. Of those that a mesh axis runs over, the one named last changes fastest.
Arguments:
- coords: int32 [8, 262144], P(None, ('rows', 'cols')), may hold values from 0 to 4095
- probes: float32 [64, 262144], P(None, ('rows', 'cols')), may hold values from -6 to 6
- lengthscales: float32 [8], replicated, may hold values from 0.15 to 0.25
- amplitude: float32 [1], replicated, may hold values from 0.1 to 0.3
- landmarks: float32 [254, 8, 128], replicated, may hold values from 0 to 1
- coupling: float32 [128, 128], replicated, may hold values from -0.5 to 0.5
Outputs:
- products: float32 [2, 64, 262144], P(None, None, ('rows', 'cols'))
All inputs are finite; a program needn't handle non-finite values.
Results may differ from a plain program's by a relative error of at most 0.0025.
Values may be sent and summed in bfloat16 or wider, within the bound.
No kernel may reach another device: no remote copies, remote signals or barrier semaphores. Data moves between devices by JAX's collectives and lax.ppermute only.
A program may use at most 64 MiB of HBM per device.

v0:
```python
import jax
import jax.numpy as jnp
from jax import lax
from jax.sharding import PartitionSpec as P


def over_pieces(array, axis):
    return lax.all_gather(array, axis).sum(0)


def swapped(array, axis, apart):
    return lax.ppermute(array, axis, [(i, i ^ 1 << apart) for i in range(lax.axis_size(axis))])


def pair_squares(left_points, right_points):
    squared = jnp.zeros((left_points.shape[1], right_points.shape[1]), jnp.float32)
    for component in range(left_points.shape[0]):
        offset = left_points[component][:, None] - right_points[component][None, :]
        squared = squared + offset * offset
    return squared


def on_device(coords, probes, lengthscales, amplitude, landmarks, coupling):
    highest = lax.Precision.HIGHEST
    inverse_scale = 1.0 / lengthscales
    scaled = coords.astype(jnp.float32) * (1.0 / 4096.0) * inverse_scale[:, None]
    strength = amplitude[0]
    signs_half = probes.astype(jnp.bfloat16)
    width = coords.shape[1]
    groups = lax.axis_size("cols")
    rows_index = lax.axis_index("rows")
    levels = lax.axis_size("rows").bit_length() - 1
    leaf_points = lax.all_gather(scaled, "cols", axis=1, tiled=True)
    leaf_signs = lax.all_gather(signs_half, "cols", axis=1, tiled=True)
    accumulated = jnp.zeros((2, probes.shape[0], width), jnp.float32)
    for row_block in range(groups):
        block_points = leaf_points[:, row_block * width : (row_block + 1) * width]
        block_signs = leaf_signs[:, row_block * width : (row_block + 1) * width]
        squared = pair_squares(block_points, scaled)
        kernel = strength * jnp.exp(-0.5 * squared)
        kernel_half = kernel.astype(jnp.bfloat16)
        slope_half = (kernel * squared).astype(jnp.bfloat16)
        accumulated = accumulated + jnp.stack(
            [
                jnp.dot(block_signs, kernel_half, preferred_element_type=jnp.float32),
                jnp.dot(block_signs, slope_half, preferred_element_type=jnp.float32),
            ]
        )
    result = accumulated
    factor_list = []
    dfactor_list = []
    for level in range(levels):
        depth = levels - level
        node = jnp.right_shift(rows_index, level)
        chosen = lax.dynamic_index_in_dim(landmarks, 2**depth - 2 + node, 0, keepdims=False)
        squared = pair_squares(scaled, chosen * inverse_scale[:, None])
        factor = strength * jnp.exp(-0.5 * squared)
        factor_list.append(factor)
        dfactor_list.append(factor * squared)
    factor_stack = jnp.stack(factor_list)
    dfactor_stack = jnp.stack(dfactor_list)
    own_project = jnp.einsum("pn,lnr->lpr", probes, factor_stack, precision=highest)
    own_dproject = jnp.einsum("pn,lnr->lpr", probes, dfactor_stack, precision=highest)
    projections = over_pieces(jnp.stack([own_project, own_dproject], axis=1), "cols")
    siblings = []
    pending = projections
    for level in range(levels):
        partner = swapped(pending[level:], "rows", level)
        siblings.append(partner[0])
        pending = pending.at[level + 1 :].add(partner[1:])
    for level in range(levels):
        sibling_sums = siblings[level]
        is_left = jnp.right_shift(rows_index, level) & 1 == 0
        core = jnp.where(is_left, coupling.T, coupling)
        first = jnp.dot(sibling_sums[0], core, precision=highest)
        second = jnp.dot(sibling_sums[1], core, precision=highest)
        value = jnp.dot(first, factor_stack[level].T, precision=highest)
        slope = jnp.dot(first, dfactor_stack[level].T, precision=highest) + jnp.dot(
            second, factor_stack[level].T, precision=highest
        )
        result = result + jnp.stack([value, slope])
    return result


def solution(mesh):
    in_specs = (P(None, ("rows", "cols")), P(None, ("rows", "cols")), P(), P(), P(), P())
    out_specs = P(None, None, ("rows", "cols"))
    return jax.shard_map(
        on_device, mesh=mesh, in_specs=in_specs, out_specs=out_specs, check_vma=False
    )
```

profile of v0, /device:TPU:1, one launch (start us, length us, event | category | flops | bytes accessed | tf_op | source)
XLA Modules:
  0.0 196.0 jit_solution(11825295575556073980)
XLA Ops:
  14.0 1.2 convolution_bitcast_fusion
  15.2 1.2 convolution_bitcast_fusion.1
  17.2 20.6 %all_gather.12 = f32[8,2048]{1,0:T(8,128)S(1)} all-gather(f32[8,512]{1,0:T(8,128)S(1)} %convert_multiply_fusion), channel_id=1, replica_groups=mesh['rows'=128,'cols'=4] {'cols'}, dimensions={1}, use_global_device_ids=true | all-gather | bytes 81920 | tf_op jit(solution)/shard_map/all_gather | solution.py:33
  37.9 15.4 %all_gather.13 = bf16[64,2048]{1,0:T(8,128)(2,1)S(1)} all-gather(bf16[64,512]{1,0:T(8,128)(2,1)S(1)} %convert_element_type.32), channel_id=1, replica_groups=mesh['rows'=128,'cols'=4] {'cols'}, dimensions={1}, use_global_device_ids=true | all-gather | bytes 327680 | tf_op jit(solution)/shard_map/all_gather | solution.py:34
  54.4 1.2 convolution_bitcast_fusion.2
  55.6 1.1 convolution_bitcast_fusion.5
  56.8 1.2 convolution_bitcast_fusion.4
  58.0 1.1 convolution_bitcast_fusion.7
  59.2 1.2 convolution_bitcast_fusion.6
  60.4 13.1 %all-gather.3.cloned.1.call-done = f32[28,2,64,128]{3,2,0,1:T(8,128)} async-done(((f32[7,2,64,128]{3,2,0,1:T(8,128)}), f32[28,2,64,128]{3,2,0,1:T(8,128)}) %all-gather.3.cloned.1.call-update) | async-done | bytes 1835024 | tf_op jit(solution)/shard_map/all_gather | solution.py:8
  73.5 1.7 reduce_sum.9
  75.2 2.0 %collective-permute-start = (f32[7,2,64,128]{3,2,0,1:T(8,128)S(1)}, f32[7,2,64,128]{3,2,0,1:T(8,128)S(1)}, u32[]{:S(2)}, u32[]{:S(2)}) collective-permute-start(f32[7,2,64,128]{3,2,0,1:T(8,128)S(1)} %reduce_sum.9), channel_id=1, source_target_pairs={{0,4},{4,0},{8,12},{12,8},{16,20},{20,16},{24,28},{28,24},{32,36},... | collective-permute-start | bytes 1376264 | tf_op jit(solution)/shard_map/ppermute | solution.py:12
  78.5 1.2 convolution_bitcast_fusion.8
  79.7 9.2 %collective-permute-done = f32[7,2,64,128]{3,2,0,1:T(8,128)S(1)} collective-permute-done((f32[7,2,64,128]{3,2,0,1:T(8,128)S(1)}, f32[7,2,64,128]{3,2,0,1:T(8,128)S(1)}, u32[]{:S(2)}, u32[]{:S(2)}) %collective-permute-start) | collective-permute-done | bytes 458784 | tf_op jit(solution)/shard_map/ppermute | solution.py:12
  88.9 3.8 %collective-permute-start.1 = (f32[6,2,64,128]{3,2,0,1:T(8,128)S(1)}, f32[6,2,64,128]{3,2,0,1:T(8,128)S(1)}, u32[]{:S(2)}, u32[]{:S(2)}) collective-permute-start(f32[6,2,64,128]{3,2,0,1:T(8,128)S(1)} %slice_add_fusion), channel_id=1, source_target_pairs={{0,8},{4,12},{8,0},{12,4},{16,24},{20,28},{24,16},{28,20},{32,40},... | collective-permute-start | bytes 1179656 | tf_op jit(solution)/shard_map/ppermute | solution.py:12
  96.1 5.7 %collective-permute-done.1 = f32[6,2,64,128]{3,2,0,1:T(8,128)S(1)} collective-permute-done((f32[6,2,64,128]{3,2,0,1:T(8,128)S(1)}, f32[6,2,64,128]{3,2,0,1:T(8,128)S(1)}, u32[]{:S(2)}, u32[]{:S(2)}) %collective-permute-start.1) | collective-permute-done | bytes 393248 | tf_op jit(solution)/shard_map/ppermute | solution.py:12
  101.9 6.0 %collective-permute-start.2 = (f32[5,2,64,128]{3,2,0,1:T(8,128)S(1)}, f32[5,2,64,128]{3,2,0,1:T(8,128)S(1)}, u32[]{:S(2)}, u32[]{:S(2)}) collective-permute-start(f32[5,2,64,128]{3,2,0,1:T(8,128)S(1)} %slice_add_fusion.1), channel_id=1, source_target_pairs={{0,16},{4,20},{8,24},{12,28},{16,0},{20,4},{24,8},{28,12},{32,48},... | collective-permute-start | bytes 983048 | tf_op jit(solution)/shard_map/ppermute | solution.py:12
  111.2 2.7 %collective-permute-done.2 = f32[5,2,64,128]{3,2,0,1:T(8,128)S(1)} collective-permute-done((f32[5,2,64,128]{3,2,0,1:T(8,128)S(1)}, f32[5,2,64,128]{3,2,0,1:T(8,128)S(1)}, u32[]{:S(2)}, u32[]{:S(2)}) %collective-permute-start.2) | collective-permute-done | bytes 327712 | tf_op jit(solution)/shard_map/ppermute | solution.py:12
  114.0 7.9 %collective-permute-start.3 = (f32[4,2,64,128]{3,2,0,1:T(8,128)S(1)}, f32[4,2,64,128]{3,2,0,1:T(8,128)S(1)}, u32[]{:S(2)}, u32[]{:S(2)}) collective-permute-start(f32[4,2,64,128]{3,2,0,1:T(8,128)S(1)} %slice_add_fusion.2), channel_id=1, source_target_pairs={{0,32},{4,36},{8,40},{12,44},{16,48},{20,52},{24,56},{28,60},{32,0... | collective-permute-start | bytes 786440 | tf_op jit(solution)/shard_map/ppermute | solution.py:12
  125.2 9.0 %collective-permute-done.3 = f32[4,2,64,128]{3,2,0,1:T(8,128)S(1)} collective-permute-done((f32[4,2,64,128]{3,2,0,1:T(8,128)S(1)}, f32[4,2,64,128]{3,2,0,1:T(8,128)S(1)}, u32[]{:S(2)}, u32[]{:S(2)}) %collective-permute-start.3) | collective-permute-done | bytes 262176 | tf_op jit(solution)/shard_map/ppermute | solution.py:12
  134.3 19.6 %collective-permute-start.4 = (f32[3,2,64,128]{3,2,0,1:T(8,128)S(1)}, f32[3,2,64,128]{3,2,0,1:T(8,128)S(1)}, u32[]{:S(2)}, u32[]{:S(2)}) collective-permute-start(f32[3,2,64,128]{3,2,0,1:T(8,128)S(1)} %slice_add_fusion.3), channel_id=1, source_target_pairs={{0,64},{4,68},{8,72},{12,76},{16,80},{20,84},{24,88},{28,92},{32,9... | collective-permute-start | bytes 589832 | tf_op jit(solution)/shard_map/ppermute | solution.py:12
  157.3 13.0 %collective-permute-done.4 = f32[3,2,64,128]{3,2,0,1:T(8,128)S(1)} collective-permute-done((f32[3,2,64,128]{3,2,0,1:T(8,128)S(1)}, f32[3,2,64,128]{3,2,0,1:T(8,128)S(1)}, u32[]{:S(2)}, u32[]{:S(2)}) %collective-permute-start.4) | collective-permute-done | bytes 196640 | tf_op jit(solution)/shard_map/ppermute | solution.py:12
  170.3 3.4 %collective-permute-start.5 = (f32[2,2,64,128]{3,2,0,1:T(8,128)S(1)}, f32[2,2,64,128]{3,2,0,1:T(8,128)S(1)}, u32[]{:S(2)}, u32[]{:S(2)}) collective-permute-start(f32[2,2,64,128]{3,2,0,1:T(8,128)S(1)} %slice_add_fusion.4), channel_id=1, source_target_pairs={{0,128},{4,132},{8,136},{12,140},{16,144},{20,148},{24,152},{28,15... | collective-permute-start | bytes 393224 | tf_op jit(solution)/shard_map/ppermute | solution.py:12
  177.1 4.3 %collective-permute-start.6 = (f32[1,2,64,128]{3,2,0,1:T(8,128)S(1)}, f32[1,2,64,128]{3,2,0,1:T(8,128)S(1)}, u32[]{:S(2)}, u32[]{:S(2)}) collective-permute-start(f32[1,2,64,128]{3,2,0,1:T(8,128)S(1)} %slice_add_fusion.5), channel_id=1, source_target_pairs={{0,256},{4,260},{8,264},{12,268},{16,272},{20,276},{24,280},{28,28... | collective-permute-start | bytes 196616 | tf_op jit(solution)/shard_map/ppermute | solution.py:12
  (72 shorter events, 34.5 us)
Async XLA Ops:
  6.5 67.0 %all-gather.3.cloned.1.call-start = ((), (), s32[]{:S(2)}) async-start(), calls=%async_computation | async-start | bytes 2293760 | tf_op jit(solution)/shard_map/all_gather | solution.py:8
  10.2 3.8 %copy-start.1 = (f32[64,512]{1,0:T(8,128)S(1)}, f32[64,512]{1,0:T(8,128)}, u32[]{:S(2)}) copy-start(f32[64,512]{1,0:T(8,128)} %param.19) | copy-start | bytes 393220
  75.2 13.7 %collective-permute-start = (f32[7,2,64,128]{3,2,0,1:T(8,128)S(1)}, f32[7,2,64,128]{3,2,0,1:T(8,128)S(1)}, u32[]{:S(2)}, u32[]{:S(2)}) collective-permute-start(f32[7,2,64,128]{3,2,0,1:T(8,128)S(1)} %reduce_sum.9), channel_id=1, source_target_pairs={{0,4},{4,0},{8,12},{12,8},{16,20},{20,16},{24,28},{28,24},{32,36},... | collective-permute-start | bytes 1376264 | tf_op jit(solution)/shard_map/ppermute | solution.py:12
  77.2 1.2 copy-start
  88.9 12.9 %collective-permute-start.1 = (f32[6,2,64,128]{3,2,0,1:T(8,128)S(1)}, f32[6,2,64,128]{3,2,0,1:T(8,128)S(1)}, u32[]{:S(2)}, u32[]{:S(2)}) collective-permute-start(f32[6,2,64,128]{3,2,0,1:T(8,128)S(1)} %slice_add_fusion), channel_id=1, source_target_pairs={{0,8},{4,12},{8,0},{12,4},{16,24},{20,28},{24,16},{28,20},{32,40},... | collective-permute-start | bytes 1179656 | tf_op jit(solution)/shard_map/ppermute | solution.py:12
  101.9 12.1 %collective-permute-start.2 = (f32[5,2,64,128]{3,2,0,1:T(8,128)S(1)}, f32[5,2,64,128]{3,2,0,1:T(8,128)S(1)}, u32[]{:S(2)}, u32[]{:S(2)}) collective-permute-start(f32[5,2,64,128]{3,2,0,1:T(8,128)S(1)} %slice_add_fusion.1), channel_id=1, source_target_pairs={{0,16},{4,20},{8,24},{12,28},{16,0},{20,4},{24,8},{28,12},{32,48},... | collective-permute-start | bytes 983048 | tf_op jit(solution)/shard_map/ppermute | solution.py:12
  114.0 20.3 %collective-permute-start.3 = (f32[4,2,64,128]{3,2,0,1:T(8,128)S(1)}, f32[4,2,64,128]{3,2,0,1:T(8,128)S(1)}, u32[]{:S(2)}, u32[]{:S(2)}) collective-permute-start(f32[4,2,64,128]{3,2,0,1:T(8,128)S(1)} %slice_add_fusion.2), channel_id=1, source_target_pairs={{0,32},{4,36},{8,40},{12,44},{16,48},{20,52},{24,56},{28,60},{32,0... | collective-permute-start | bytes 786440 | tf_op jit(solution)/shard_map/ppermute | solution.py:12
  134.3 36.0 %collective-permute-start.4 = (f32[3,2,64,128]{3,2,0,1:T(8,128)S(1)}, f32[3,2,64,128]{3,2,0,1:T(8,128)S(1)}, u32[]{:S(2)}, u32[]{:S(2)}) collective-permute-start(f32[3,2,64,128]{3,2,0,1:T(8,128)S(1)} %slice_add_fusion.3), channel_id=1, source_target_pairs={{0,64},{4,68},{8,72},{12,76},{16,80},{20,84},{24,88},{28,92},{32,9... | collective-permute-start | bytes 589832 | tf_op jit(solution)/shard_map/ppermute | solution.py:12
  170.3 6.8 %collective-permute-start.5 = (f32[2,2,64,128]{3,2,0,1:T(8,128)S(1)}, f32[2,2,64,128]{3,2,0,1:T(8,128)S(1)}, u32[]{:S(2)}, u32[]{:S(2)}) collective-permute-start(f32[2,2,64,128]{3,2,0,1:T(8,128)S(1)} %slice_add_fusion.4), channel_id=1, source_target_pairs={{0,128},{4,132},{8,136},{12,140},{16,144},{20,148},{24,152},{28,15... | collective-permute-start | bytes 393224 | tf_op jit(solution)/shard_map/ppermute | solution.py:12
  177.1 7.7 %collective-permute-start.6 = (f32[1,2,64,128]{3,2,0,1:T(8,128)S(1)}, f32[1,2,64,128]{3,2,0,1:T(8,128)S(1)}, u32[]{:S(2)}, u32[]{:S(2)}) collective-permute-start(f32[1,2,64,128]{3,2,0,1:T(8,128)S(1)} %slice_add_fusion.5), channel_id=1, source_target_pairs={{0,256},{4,260},{8,264},{12,268},{16,272},{20,276},{24,280},{28,28... | collective-permute-start | bytes 196616 | tf_op jit(solution)/shard_map/ppermute | solution.py:12
Sparse Core Ops, SparseCore 0:
  17.3 56.1 all-gather.2
where the time goes:
time: 197 us; the launch traced here: 196 us
  waiting for transfers between devices  52.7 us (27%)
  starting transfers between devices  47.1 us (24%)
  blocking collectives  36 us (18%)
  matrix products  35.1 us (18%)
  between operations  14.5 us (7%)
  other arithmetic  10.3 us (5%)
    ppermute x7, starting transfers between devices, swapped(): lax.ppermute(array, axis, [(i, i ^ 1 << apart) for i in range(lax.axis_si...  47.1 us
    ppermute x7, waiting for transfers between devices, swapped(): lax.ppermute(array, axis, [(i, i ^ 1 << apart) for i in range(lax.axis_si...  39.6 us
    all_gather x1, blocking collectives, on_device(): leaf_points = lax.all_gather(scaled, 'cols', axis=1, tiled=True)  20.6 us
    all_gather x1, blocking collectives, on_device(): leaf_signs = lax.all_gather(signs_half, 'cols', axis=1, tiled=True)  15.4 us
    all_gather x1, waiting for transfers between devices, over_pieces(): return lax.all_gather(array, axis).sum(0)  13.1 us
    dot_general x7, matrix products, on_device(): jnp.dot(second, factor_stack[level].T, precision=highest)  6.89 us
    dot_general x7, matrix products, on_device(): jnp.dot(first, dfactor_stack[level].T, precision=highest)  6.89 us
    dot_general x7, matrix products, on_device(): value = jnp.dot(first, factor_stack[level].T, precision=highest)  6.89 us
  transfers between devices with their start and end apart: 8, of which 6 were waited for; matrix products, arithmetic and copies ran while one was open for 15% of the time, Pallas kernels for 0%

commit v1 on v0

v1 whole, which is shorter than its diff:
```python
import functools
import math

import jax
import jax.numpy as jnp
from jax import lax
from jax.experimental import pallas as pl
from jax.experimental.pallas import tpu as pltpu
from jax.sharding import Mesh, PartitionSpec as P

LEVELS = 7
PROBES = 64
RANK = 128
HALF = RANK // 2
QUARTER = PROBES // 4
SPAN = 128
WIDTH = 512
TRANSFER = 80
LANES = 1024
BLOCK = 256
ROOT = math.sqrt(math.log2(math.e))
TWO_LN2 = 2.0 * math.log(2.0)
F32 = jnp.float32
BF16 = jnp.bfloat16
VMEM = pl.BlockSpec(memory_space=pltpu.VMEM)
SMEM = pl.BlockSpec(memory_space=pltpu.SMEM)


def cost(flops, moved):
    return pl.CostEstimate(flops=flops, bytes_accessed=moved, transcendentals=0)


def split3(value):
    first = value.astype(BF16).astype(F32)
    rest = value - first
    second = rest.astype(BF16).astype(F32)
    third = (rest - second).astype(BF16).astype(F32)
    return first, second, third


def inverse_scales(scales_ref):
    row = lax.broadcasted_iota(jnp.int32, (8, 128), 0)
    held = jnp.full((8, 128), scales_ref[0], F32)
    for k in range(1, 8):
        held = jnp.where(row == k, scales_ref[k], held)
    return (ROOT / held)[:, :1]


def norms(value):
    return -0.5 * jnp.sum(value * value, axis=0, keepdims=True)


def stacked(parts, rows):
    width = parts[0].shape[1]
    index = lax.broadcasted_iota(jnp.int32, (8, width), 0)
    held = jnp.zeros((8, width), F32)
    for k, row in enumerate(rows):
        held = jnp.where(index == k, row, held)
    zeros = jnp.zeros((SPAN - 56, width), F32)
    return jnp.concatenate(list(parts) + [held, zeros], axis=0)


def left_form(value, extra):
    one, two, three = split3(value)
    n1, n2, n3 = split3(norms(value) + extra)
    return stacked((one, one, two, one, three, two), (1.0, 1.0, 1.0, n1, n2, n3))


def right_form(value, extra):
    one, two, three = split3(value)
    n1, n2, n3 = split3(norms(value) + extra)
    return stacked((one, two, one, three, one, two), (n1, n2, n3, 1.0, 1.0, 1.0))


def points_of(message, inverse):
    high = message[PROBES : PROBES + 8, :].astype(F32)
    low = message[PROBES + 8 : PROBES + 16, :].astype(F32)
    return ((high * 64.0 + low) * (1.0 / 4096.0) - 0.5) * inverse


def kernel_pair(exponent, log_strength):
    kern = jnp.exp2(exponent)
    return kern, kern * (TWO_LN2 * log_strength - TWO_LN2 * exponent)


def halved(value):
    top = value.astype(BF16)
    return top, (value - top.astype(F32)).astype(BF16)


def log2_strength(strength_ref):
    return jnp.log(jnp.full((1, 128), strength_ref[0], F32))[:, :1] * math.log2(math.e)


def prepare_kernel(coords_ref, probes_ref, out_ref):
    coords = coords_ref[...]
    high = jnp.right_shift(coords, 6)
    low = coords - high * 64
    out_ref[0:PROBES, :] = probes_ref[...].astype(BF16)
    both = jnp.concatenate([high.astype(F32), low.astype(F32)], axis=0)
    out_ref[PROBES:TRANSFER, :] = both.astype(BF16)


def accumulate(message_ref, inverse, right, log_strength, held_k, held_s, fresh):
    message = message_ref[...]
    left = left_form(points_of(message, inverse), 0.0).T.astype(BF16)
    for block in range(WIDTH // BLOCK):
        rows = left[block * BLOCK : (block + 1) * BLOCK, :]
        signs = message[0:PROBES, block * BLOCK : (block + 1) * BLOCK]
        for at in range(0, LANES, BLOCK):
            exponent = jnp.dot(rows, right[:, at : at + BLOCK], preferred_element_type=F32)
            sums = []
            for value in kernel_pair(exponent, log_strength):
                top, rest = halved(value)
                total = jnp.dot(signs, top, preferred_element_type=F32)
                if at >= WIDTH:
                    total = total + jnp.dot(signs, rest, preferred_element_type=F32)
                sums.append(total)
            add_k, add_s = sums
            if fresh and block == 0:
                held_k[:, at : at + BLOCK] = add_k
                held_s[:, at : at + BLOCK] = add_s
            else:
                held_k[:, at : at + BLOCK] += add_k
                held_s[:, at : at + BLOCK] += add_s


def near_kernel(
    own_ref, other_ref, scales_ref, strength_ref, marks_ref,
    held_ref, right_ref, factor_ref, marks_buf, sem,
):
    row = lax.axis_index("x") * 32 + lax.axis_index("z") * 4 + lax.axis_index("y")
    core = lax.axis_index("c")
    copies = []
    for level in range(LEVELS):
        node = 2 ** (LEVELS - level) - 2 + jnp.right_shift(row, level)
        copies.append(pltpu.make_async_copy(marks_ref.at[node], marks_buf.at[level], sem.at[level]))
    for copy in copies:
        copy.start()
    inverse = inverse_scales(scales_ref)
    log_strength = log2_strength(strength_ref)
    own = points_of(own_ref[...], inverse)
    for copy in copies:
        copy.wait()
    marks = [(marks_buf[level] - 0.5) * inverse for level in range(LEVELS)]
    halves = [jnp.where(core == 0, mark[:, :HALF], mark[:, HALF:]) for mark in marks]
    halves.append(jnp.zeros((8, HALF), F32))
    columns = jnp.concatenate([own] + halves, axis=1)
    right = right_form(columns, log_strength).astype(BF16)
    right_ref[...] = right
    accumulate(own_ref, inverse, right, log_strength, held_ref.at[0], held_ref.at[1], True)
    accumulate(other_ref, inverse, right, log_strength, held_ref.at[0], held_ref.at[1], False)
    own_right = right[:, :WIDTH]
    for level in range(LEVELS):
        turned = left_form(marks[level], 0.0).T.astype(BF16)
        exponent = jnp.dot(turned, own_right, preferred_element_type=F32)
        kern, slope = kernel_pair(exponent, log_strength)
        factor_ref[0, level * RANK : (level + 1) * RANK, :] = kern.astype(BF16)
        factor_ref[1, level * RANK : (level + 1) * RANK, :] = slope.astype(BF16)


def far_kernel(
    far_ref, cross_ref, scales_ref, strength_ref, held_ref, right_ref,
    diagonal_ref, plane_ref, low_ref, sums,
):
    x = lax.axis_index("x")
    y = lax.axis_index("y")
    inverse = inverse_scales(scales_ref)
    log_strength = log2_strength(strength_ref)
    right = right_ref[...]
    sums[...] = held_ref[...]
    accumulate(far_ref, inverse, right, log_strength, sums.at[0], sums.at[1], False)
    accumulate(cross_ref, inverse, right, log_strength, sums.at[0], sums.at[1], False)
    diagonal_ref[...] = sums[:, :, :WIDTH]
    units = []
    for level in range(LEVELS):
        at = WIDTH + level * HALF
        pair = [sums[0, :, at : at + HALF], sums[1, :, at : at + HALF]]
        units.append(jnp.concatenate(pair, axis=1))
    blank = jnp.zeros((2 * QUARTER, 128), F32)
    for at in range(4):
        part = slice(at * QUARTER, (at + 1) * QUARTER)
        mine = jnp.concatenate([units[2][part], units[3][part], units[4][part]], axis=0)
        plane_ref[x * 4 + at] = mine
        for apart, level in ((1, 5), (2, 6), (3, 6)):
            plane_ref[jnp.bitwise_xor(x, apart) * 4 + at] = jnp.concatenate([units[level][part], blank], axis=0)
    low_ref[y] = jnp.zeros((PROBES, 128), F32)
    for apart, level in ((1, 0), (2, 1), (3, 1)):
        low_ref[jnp.bitwise_xor(y, apart)] = units[level]


def plane_kernel(got_ref, out_ref):
    x = lax.axis_index("x")
    z = lax.axis_index("z")

    def total(apart, rows):
        start = jnp.bitwise_xor(x, apart) * 4
        parts = [got_ref[start + at, rows] for at in range(4)]
        return (parts[0] + parts[1]) + (parts[2] + parts[3])

    low, middle, high = slice(0, 16), slice(16, 32), slice(32, 48)
    sums = [total(0, low), total(0, middle), total(0, high)]
    five = total(1, low)
    six = total(2, low) + total(3, low)
    chosen = [jnp.zeros((QUARTER, 128), F32)] + sums
    for apart in range(8):
        which = apart.bit_length()
        out_ref[jnp.bitwise_xor(z, apart)] = jnp.concatenate([chosen[which], five, six], axis=0)


def depth_kernel(got_ref, low_ref, out_ref):
    z = lax.axis_index("z")

    def piece(apart, start):
        return got_ref[jnp.bitwise_xor(z, apart), start : start + QUARTER]

    two = piece(1, 0)
    three = piece(2, 0) + piece(3, 0)
    four = (piece(4, 0) + piece(5, 0)) + (piece(6, 0) + piece(7, 0))
    found = [two, three, four]
    for start in (QUARTER, 2 * QUARTER):
        parts = [piece(apart, start) for apart in range(8)]
        while len(parts) > 1:
            parts = [a + b for a, b in zip(parts[::2], parts[1::2])]
        found.append(parts[0])
    packed = jnp.concatenate(found, axis=0)
    for at in range(4):
        for core in range(2):
            out_ref[2 * at + core, 0:PROBES] = low_ref[at]
            out_ref[2 * at + core, PROBES:] = packed


def final_kernel(got_ref, factor_ref, coupling_ref, diagonal_ref, out_ref, sibling):
    y = lax.axis_index("y")
    row = lax.axis_index("x") * 32 + lax.axis_index("z") * 4 + y
    for core in range(2):
        lanes = slice(core * 128, core * 128 + 128)
        sibling[0:PROBES, lanes] = got_ref[jnp.bitwise_xor(y, 1) * 2 + core, 0:PROBES]
        pair = got_ref[jnp.bitwise_xor(y, 2) * 2 + core, 0:PROBES]
        pair = pair + got_ref[jnp.bitwise_xor(y, 3) * 2 + core, 0:PROBES]
        sibling[PROBES : 2 * PROBES, lanes] = pair
        for level in range(2, LEVELS):
            for at in range(4):
                start = level * PROBES + at * QUARTER
                source = PROBES + (level - 2) * QUARTER
                sibling[start : start + QUARTER, lanes] = got_ref[2 * at + core, source : source + QUARTER]
    coupling = coupling_ref[...]
    blank = jnp.zeros((HALF, RANK), F32)

    def spread(core_matrix):
        rows = []
        for core in range(2):
            part = core_matrix[core * HALF : (core + 1) * HALF, :]
            rows.append(jnp.concatenate([part, blank], axis=1))
            rows.append(jnp.concatenate([blank, part], axis=1))
        whole = jnp.concatenate(rows, axis=0)
        return halved(whole)

    values, remainders = halved(sibling[...])
    results = []
    for matrix in (coupling.T, coupling):
        top, rest = spread(matrix)
        results.append(
            jnp.dot(values, top, preferred_element_type=F32)
            + jnp.dot(values, rest, preferred_element_type=F32)
            + jnp.dot(remainders, top, preferred_element_type=F32)
        )
    heads = []
    for level in range(LEVELS):
        rows = slice(level * PROBES, (level + 1) * PROBES)
        left = jnp.bitwise_and(jnp.right_shift(row, level), 1) == 0
        heads.append(jnp.where(left, results[0][rows], results[1][rows]))
    firsts = jnp.concatenate([head[:, :RANK] for head in heads], axis=1)
    seconds = jnp.concatenate([head[:, RANK:] for head in heads], axis=1)
    top, rest = halved(jnp.concatenate([firsts, seconds], axis=0))
    stack = jnp.concatenate([top, rest], axis=0)
    on_kern = jnp.dot(stack, factor_ref[0], preferred_element_type=F32)
    pair = jnp.concatenate([top[:PROBES], rest[:PROBES]], axis=0)
    on_slope = jnp.dot(pair, factor_ref[1], preferred_element_type=F32)
    on_kern = on_kern[: 2 * PROBES] + on_kern[2 * PROBES :]
    on_slope = on_slope[:PROBES] + on_slope[PROBES:]
    out_ref[0] = diagonal_ref[0] + on_kern[:PROBES]
    out_ref[1] = diagonal_ref[1] + (on_kern[PROBES:] + on_slope)


def swap(value, axis):
    return lax.ppermute(value, axis, [(0, 1), (1, 0)])


def exchange(value, axes):
    return lax.all_to_all(value, axes, 0, 0, tiled=True)


def on_device(coords, probes, lengthscales, amplitude, landmarks, coupling):
    message = pl.pallas_call(
        prepare_kernel,
        out_shape=jax.ShapeDtypeStruct((TRANSFER, WIDTH), BF16),
        in_specs=[VMEM, VMEM],
        out_specs=VMEM,
        cost_estimate=cost(10**5, 2 * 10**5),
        name="prepare",
    )(coords, probes)
    far = swap(message, "h")
    other = swap(message, "c")
    held, right, factor = pl.pallas_call(
        near_kernel,
        out_shape=(
            jax.ShapeDtypeStruct((2, PROBES, LANES), F32),
            jax.ShapeDtypeStruct((SPAN, LANES), BF16),
            jax.ShapeDtypeStruct((2, LEVELS * RANK, WIDTH), BF16),
        ),
        in_specs=[VMEM, VMEM, SMEM, SMEM, pl.BlockSpec(memory_space=pl.ANY)],
        out_specs=(VMEM, VMEM, VMEM),
        scratch_shapes=[pltpu.VMEM((LEVELS, 8, RANK), F32), pltpu.SemaphoreType.DMA((LEVELS,))],
        cost_estimate=cost(2 * 10**9, 3 * 10**6),
        name="near",
    )(message, other, lengthscales, amplitude, landmarks)
    cross = swap(far, "c")
    diagonal, plane, low = pl.pallas_call(
        far_kernel,
        out_shape=(
            jax.ShapeDtypeStruct((2, PROBES, WIDTH), F32),
            jax.ShapeDtypeStruct((16, 3 * QUARTER, 128), F32),
            jax.ShapeDtypeStruct((4, PROBES, 128), F32),
        ),
        in_specs=[VMEM, VMEM, SMEM, SMEM, VMEM, VMEM],
        out_specs=(VMEM, VMEM, VMEM),
        scratch_shapes=[pltpu.VMEM((2, PROBES, LANES), F32)],
        cost_estimate=cost(10**9, 2 * 10**6),
        name="far",
    )(far, cross, lengthscales, amplitude, held, right)
    plane = exchange(plane, ("x", "y"))
    deep = pl.pallas_call(
        plane_kernel,
        out_shape=jax.ShapeDtypeStruct((8, 3 * QUARTER, 128), F32),
        in_specs=[VMEM],
        out_specs=VMEM,
        cost_estimate=cost(10**5, 3 * 10**5),
        name="plane",
    )(plane)
    deep = exchange(deep, "z")
    wide = pl.pallas_call(
        depth_kernel,
        out_shape=jax.ShapeDtypeStruct((8, PROBES + 5 * QUARTER, 128), F32),
        in_specs=[VMEM, VMEM],
        out_specs=VMEM,
        cost_estimate=cost(10**5, 5 * 10**5),
        name="depth",
    )(deep, low)
    wide = exchange(wide, ("y", "c"))
    return pl.pallas_call(
        final_kernel,
        out_shape=jax.ShapeDtypeStruct((2, PROBES, WIDTH), F32),
        in_specs=[VMEM] * 4,
        out_specs=VMEM,
        scratch_shapes=[pltpu.VMEM((LEVELS * PROBES, 2 * RANK), F32)],
        cost_estimate=cost(10**9, 3 * 10**6),
        name="final",
    )(wide, factor, coupling, diagonal)


def solution(mesh):
    fine = Mesh(mesh.devices.reshape(4, 8, 4, 2, 2), ("x", "z", "y", "h", "c"))
    every = ("x", "z", "y", "h", "c")
    in_specs = (P(None, every), P(None, every), P(), P(), P(), P())
    return jax.shard_map(
        on_device, mesh=fine, in_specs=in_specs, out_specs=P(None, None, every), check_vma=False
    )
```

time: 197 us -> 101 us (0.51)
  waiting for transfers between devices: 52.7 us -> 0.01 us
  matrix products: 35.1 us -> 0 us
  starting transfers between devices: 47.1 us -> 23.3 us
  Pallas kernels: 0 us -> 20.4 us
  blocking collectives: 36 us -> 55.1 us
  between operations: 14.5 us -> 0.74 us
  other arithmetic: 10.3 us -> 0 us
    all_to_all x0 -> x3, blocking collectives: none -> 55.1 us  [exchange(): return lax.all_to_all(value, axes, 0, 0, tiled=True)]
    ppermute x7 -> x3, waiting for transfers between devices: 39.6 us -> 0.01 us  [swap(): return lax.ppermute(value, axis, [(0, 1), (1, 0)])]
    all_gather x2 -> x0, blocking collectives: 36 us -> none  [the longest x1 20.6 us: on_device(): leaf_points = lax.all_gather(scaled, 'cols', axis=1, tiled=True)]
    dot_general x45 -> x0, matrix products: 35.1 us -> none  [the longest x7 6.89 us: on_device(): jnp.dot(second, factor_stack[level].T, precision=highest)]
    ppermute x7 -> x3, starting transfers between devices: 47.1 us -> 23.3 us  [swap(): return lax.ppermute(value, axis, [(0, 1), (1, 0)])]
    pallas_call x0 -> x6, Pallas kernels: none -> 20.4 us  [the longest x1 6.64 us: on_device(): pl.pallas_call(near_kernel, out_shape=(jax.ShapeDtypeStruct((2, PROBES, L...]
    all_gather x1 -> x0, waiting for transfers between devices: 13.1 us -> none  [over_pieces(): return lax.all_gather(array, axis).sum(0)]
    unnamed x6 -> x0, other arithmetic: 3.73 us -> none
  transfers between devices with their start and end apart: 8 -> 3, of which waited for: 6 -> 0; matrix products, arithmetic and copies ran while one was open for 15% -> 0% of each run, Pallas kernels for 0% -> 7%
where the time goes in v1:
time: 101 us
  blocking collectives  55.1 us (55%)
  starting transfers between devices  23.3 us (23%)
  Pallas kernels  20.4 us (20%)
  local copies, waits for them, and re-layouts  1.25 us (1%)
    all_to_all x3, blocking collectives, exchange(): return lax.all_to_all(value, axes, 0, 0, tiled=True)  55.1 us
    ppermute x3, starting transfers between devices, swap(): return lax.ppermute(value, axis, [(0, 1), (1, 0)])  23.3 us
    pallas_call x1, Pallas kernels, on_device(): pl.pallas_call(near_kernel, out_shape=(jax.ShapeDtypeStruct((2, PROBES, L...  6.64 us
    pallas_call x1, Pallas kernels, on_device(): pl.pallas_call(far_kernel, out_shape=(jax.ShapeDtypeStruct((2, PROBES, WI...  5.16 us
    pallas_call x1, Pallas kernels, on_device(): pl.pallas_call(final_kernel, out_shape=jax.ShapeDtypeStruct((2, PROBES, W...  3.45 us
  transfers between devices with their start and end apart: 3, of which 0 were waited for; matrix products, arithmetic and copies ran while one was open for 0% of the time, Pallas kernels for 7%

profile of v1, /device:TPU:1, one launch (start us, length us, event | category | flops | bytes accessed | tf_op | source)
XLA Modules:
  0.0 100.7 jit_solution(14171467326619597628)
XLA Ops:
  0.0 1.6 %prepare.1.own_ref = bf16[80,512]{1,0:T(8,128)(2,1)} custom-call(s32[8,512]{1,0:T(8,128)} %coords_ref.1, f32[64,512]{1,0:T(8,128)} %probes_ref.1), custom_call_target="tpu_custom_call" | custom-call | flops 100000 | bytes 200000 | tf_op jit(solution)/shard_map/prepare/pallas_call | solution.py:295
  1.6 16.2 %collective-permute-start = (bf16[80,512]{1,0:T(8,128)(2,1)}, bf16[80,512]{1,0:T(8,128)(2,1)S(1)}, u32[]{:S(2)}, u32[]{:S(2)}) collective-permute-start(bf16[80,512]{1,0:T(8,128)(2,1)} %prepare.1.own_ref), channel_id=1, source_target_pairs={{0,2},{2,0},{1,3},{3,1},{4,6},{6,4},{5,7},{7,5},{8,10},{10,8},{9,1... | collective-permute-start | bytes 245768 | tf_op jit(solution)/shard_map/ppermute | solution.py:287
  17.8 2.9 %collective-permute-start.2 = (bf16[80,512]{1,0:T(8,128)(2,1)}, bf16[80,512]{1,0:T(8,128)(2,1)S(1)}, u32[]{:S(2)}, u32[]{:S(2)}) collective-permute-start(bf16[80,512]{1,0:T(8,128)(2,1)} %prepare.1.own_ref), channel_id=1, source_target_pairs={{0,1},{1,0},{2,3},{3,2},{4,5},{5,4},{6,7},{7,6},{8,9},{9,8},{10,11... | collective-permute-start | bytes 245768 | tf_op jit(solution)/shard_map/ppermute | solution.py:287
  21.3 0.0 collective-permute-done.far_ref
  21.4 0.0 copy-start
  21.4 4.2 %collective-permute-start.1 = (bf16[80,512]{1,0:T(8,128)(2,1)S(1)}, bf16[80,512]{1,0:T(8,128)(2,1)S(1)}, u32[]{:S(2)}, u32[]{:S(2)}) collective-permute-start(bf16[80,512]{1,0:T(8,128)(2,1)S(1)} %collective-permute-done.far_ref), channel_id=1, source_target_pairs={{0,1},{1,0},{2,3},{3,2},{4,5},{5,4},{6,7},{7,6},{8,9},{9,8},{10,11... | collective-permute-start | bytes 245768 | tf_op jit(solution)/shard_map/ppermute | solution.py:287
  25.6 0.0 collective-permute-done.2.other_ref
  25.6 0.0 copy-start.2
  25.6 0.6 copy-done.2
  26.2 6.6 %near.1 = (f32[2,64,1024]{2,1,0:T(8,128)}, bf16[128,1024]{1,0:T(8,128)(2,1)}, bf16[2,896,512]{2,1,0:T(8,128)(2,1)}) custom-call(bf16[80,512]{1,0:T(8,128)(2,1)} %prepare.1.own_ref, bf16[80,512]{1,0:T(8,128)(2,1)} %copy-done.2, f32[8]{0:T(128)} %scales_ref.3, f32[1]{0:T(128)S(6)} %copy.7.strength_ref, f32[254,8,128]{2,1,0:T(8,128)} %marks_ref.1), custom_call_target="tpu_custom_call" | custom-call | flops 2000000000 | bytes 3000000 | tf_op jit(solution)/shard_map/near/pallas_call | solution.py:305
  32.8 0.0 copy-done
  32.9 0.0 collective-permute-done.1.cross_ref
  32.9 0.0 copy-start.1
  32.9 0.6 copy-done.1
  33.5 5.2 %far.1 = (f32[2,64,512]{2,1,0:T(8,128)}, f32[16,48,128]{2,1,0:T(8,128)}, f32[4,64,128]{2,1,0:T(8,128)}) custom-call(bf16[80,512]{1,0:T(8,128)(2,1)} %copy-done, bf16[80,512]{1,0:T(8,128)(2,1)} %copy-done.1, f32[8]{0:T(128)} %scales_ref.3, f32[1]{0:T(128)S(6)} %copy.7.strength_ref, f32[2,64,1024]{2,1,0:T(8,128)} %get-tuple-element.11.held_ref, ...), custom_call_target="tpu_custom_call" | custom-call | flops 1000000000 | bytes 2000000 | tf_op jit(solution)/shard_map/far/pallas_call | solution.py:319
  38.7 14.2 %all_to_all.15.got_ref = f32[16,48,128]{2,1,0:T(8,128)} all-to-all(f32[16,48,128]{2,1,0:T(8,128)} %get-tuple-element.13), channel_id=1, replica_groups=mesh['x'=4,'z'=8,'y'=4,'h'=2,'c'=2] {'x','y'}, dimensions={0} | all-to-all | bytes 786432 | tf_op jit(solution)/shard_map/all_to_all | solution.py:291
  52.9 1.7 %plane.1 = f32[8,48,128]{2,1,0:T(8,128)} custom-call(f32[16,48,128]{2,1,0:T(8,128)} %all_to_all.15.got_ref), custom_call_target="tpu_custom_call" | custom-call | flops 100000 | bytes 300000 | tf_op jit(solution)/shard_map/plane/pallas_call | solution.py:333
  54.6 22.5 %all_to_all.16.got_ref = f32[8,48,128]{2,1,0:T(8,128)} all-to-all(f32[8,48,128]{2,1,0:T(8,128)} %plane.1), channel_id=1, replica_groups=mesh['x'=4,'z'=8,'y'=4,'h'=2,'c'=2] {'z'}, dimensions={0} | all-to-all | bytes 393216 | tf_op jit(solution)/shard_map/all_to_all | solution.py:291
  77.0 1.8 %depth.1 = f32[8,144,128]{2,1,0:T(8,128)} custom-call(f32[8,48,128]{2,1,0:T(8,128)} %all_to_all.16.got_ref, f32[4,64,128]{2,1,0:T(8,128)} %get-tuple-element.14.low_ref), custom_call_target="tpu_custom_call" | custom-call | flops 100000 | bytes 500000 | tf_op jit(solution)/shard_map/depth/pallas_call | solution.py:342
  78.9 18.4 %all_to_all.17.got_ref = f32[8,144,128]{2,1,0:T(8,128)} all-to-all(f32[8,144,128]{2,1,0:T(8,128)} %depth.1), channel_id=1, replica_groups=mesh['x'=4,'z'=8,'y'=4,'h'=2,'c'=2] {'y','c'}, dimensions={0} | all-to-all | bytes 1179648 | tf_op jit(solution)/shard_map/all_to_all | solution.py:291
  97.3 3.4 %final.1 = f32[2,64,512]{2,1,0:T(8,128)} custom-call(f32[8,144,128]{2,1,0:T(8,128)} %all_to_all.17.got_ref, bf16[2,896,512]{2,1,0:T(8,128)(2,1)} %get-tuple-element.15.factor_ref, f32[128,128]{1,0:T(8,128)} %coupling_ref.1, f32[2,64,512]{2,1,0:T(8,128)} %get-tuple-element.16.diagonal_ref), custom_call_target="tpu_custom_call" | custom-call | flops 1000000000 | bytes 3000000 | tf_op jit(solution)/shard_map/final/pallas_call | solution.py:351
Async XLA Ops:
  1.6 19.8 %collective-permute-start = (bf16[80,512]{1,0:T(8,128)(2,1)}, bf16[80,512]{1,0:T(8,128)(2,1)S(1)}, u32[]{:S(2)}, u32[]{:S(2)}) collective-permute-start(bf16[80,512]{1,0:T(8,128)(2,1)} %prepare.1.own_ref), channel_id=1, source_target_pairs={{0,2},{2,0},{1,3},{3,1},{4,6},{6,4},{5,7},{7,5},{8,10},{10,8},{9,1... | collective-permute-start | bytes 245768 | tf_op jit(solution)/shard_map/ppermute | solution.py:287
  17.8 7.7 %collective-permute-start.2 = (bf16[80,512]{1,0:T(8,128)(2,1)}, bf16[80,512]{1,0:T(8,128)(2,1)S(1)}, u32[]{:S(2)}, u32[]{:S(2)}) collective-permute-start(bf16[80,512]{1,0:T(8,128)(2,1)} %prepare.1.own_ref), channel_id=1, source_target_pairs={{0,1},{1,0},{2,3},{3,2},{4,5},{5,4},{6,7},{7,6},{8,9},{9,8},{10,11... | collective-permute-start | bytes 245768 | tf_op jit(solution)/shard_map/ppermute | solution.py:287
  21.4 11.5 %copy-start = (bf16[80,512]{1,0:T(8,128)(2,1)}, bf16[80,512]{1,0:T(8,128)(2,1)S(1)}, u32[]{:S(2)}) copy-start(bf16[80,512]{1,0:T(8,128)(2,1)S(1)} %collective-permute-done.far_ref) | copy-start | bytes 245764
  21.4 11.5 %collective-permute-start.1 = (bf16[80,512]{1,0:T(8,128)(2,1)S(1)}, bf16[80,512]{1,0:T(8,128)(2,1)S(1)}, u32[]{:S(2)}, u32[]{:S(2)}) collective-permute-start(bf16[80,512]{1,0:T(8,128)(2,1)S(1)} %collective-permute-done.far_ref), channel_id=1, source_target_pairs={{0,1},{1,0},{2,3},{3,2},{4,5},{5,4},{6,7},{7,6},{8,9},{9,8},{10,11... | collective-permute-start | bytes 245768 | tf_op jit(solution)/shard_map/ppermute | solution.py:287
  25.6 0.6 copy-start.2
  32.9 0.6 copy-start.1

commit v2 on v1

--- a/solution.py
+++ b/solution.py
@@ -1,4 +1,3 @@
-import functools
 import math
 
 import jax
@@ -7,6 +6,7 @@
 from jax.experimental import pallas as pl
 from jax.experimental.pallas import tpu as pltpu
 from jax.sharding import Mesh, PartitionSpec as P
+
 
 LEVELS = 7
 PROBES = 64
@@ -23,6 +23,7 @@
 F32 = jnp.float32
 BF16 = jnp.bfloat16
 VMEM = pl.BlockSpec(memory_space=pltpu.VMEM)
+ROOM = pltpu.CompilerParams(vmem_limit_bytes=16 * 2**20)
 SMEM = pl.BlockSpec(memory_space=pltpu.SMEM)
 
 
@@ -127,22 +128,17 @@
 
 def near_kernel(
     own_ref, other_ref, scales_ref, strength_ref, marks_ref,
-    held_ref, right_ref, factor_ref, marks_buf, sem,
+    held_ref, right_ref, factor_ref,
 ):
     row = lax.axis_index("x") * 32 + lax.axis_index("z") * 4 + lax.axis_index("y")
     core = lax.axis_index("c")
-    copies = []
-    for level in range(LEVELS):
-        node = 2 ** (LEVELS - level) - 2 + jnp.right_shift(row, level)
-        copies.append(pltpu.make_async_copy(marks_ref.at[node], marks_buf.at[level], sem.at[level]))
-    for copy in copies:
-        copy.start()
     inverse = inverse_scales(scales_ref)
     log_strength = log2_strength(strength_ref)
     own = points_of(own_ref[...], inverse)
-    for copy in copies:
-        copy.wait()
-    marks = [(marks_buf[level] - 0.5) * inverse for level in range(LEVELS)]
+    marks = []
+    for level in range(LEVELS):
+        node = 2 ** (LEVELS - level) - 2 + jnp.right_shift(row, level)
+        marks.append((marks_ref[node] - 0.5) * inverse)
     halves = [jnp.where(core == 0, mark[:, :HALF], mark[:, HALF:]) for mark in marks]
     halves.append(jnp.zeros((8, HALF), F32))
     columns = jnp.concatenate([own] + halves, axis=1)
@@ -297,6 +293,7 @@
         out_shape=jax.ShapeDtypeStruct((TRANSFER, WIDTH), BF16),
         in_specs=[VMEM, VMEM],
         out_specs=VMEM,
+        compiler_params=ROOM,
         cost_estimate=cost(10**5, 2 * 10**5),
         name="prepare",
     )(coords, probes)
@@ -309,12 +306,13 @@
             jax.ShapeDtypeStruct((SPAN, LANES), BF16),
             jax.ShapeDtypeStruct((2, LEVELS * RANK, WIDTH), BF16),
         ),
-        in_specs=[VMEM, VMEM, SMEM, SMEM, pl.BlockSpec(memory_space=pl.ANY)],
+        in_specs=[VMEM, VMEM, SMEM, SMEM, VMEM],
         out_specs=(VMEM, VMEM, VMEM),
-        scratch_shapes=[pltpu.VMEM((LEVELS, 8, RANK), F32), pltpu.SemaphoreType.DMA((LEVELS,))],
+        compiler_params=ROOM,
         cost_estimate=cost(2 * 10**9, 3 * 10**6),
         name="near",
     )(message, other, lengthscales, amplitude, landmarks)
+    far, held, right = lax.optimization_barrier((far, held, right))
     cross = swap(far, "c")
     diagonal, plane, low = pl.pallas_call(
         far_kernel,
@@ -326,6 +324,7 @@
         in_specs=[VMEM, VMEM, SMEM, SMEM, VMEM, VMEM],
         out_specs=(VMEM, VMEM, VMEM),
         scratch_shapes=[pltpu.VMEM((2, PROBES, LANES), F32)],
+        compiler_params=ROOM,
         cost_estimate=cost(10**9, 2 * 10**6),
         name="far",
     )(far, cross, lengthscales, amplitude, held, right)
@@ -335,6 +334,7 @@
         out_shape=jax.ShapeDtypeStruct((8, 3 * QUARTER, 128), F32),
         in_specs=[VMEM],
         out_specs=VMEM,
+        compiler_params=ROOM,
         cost_estimate=cost(10**5, 3 * 10**5),
         name="plane",
     )(plane)
@@ -344,6 +344,7 @@
         out_shape=jax.ShapeDtypeStruct((8, PROBES + 5 * QUARTER, 128), F32),
         in_specs=[VMEM, VMEM],
         out_specs=VMEM,
+        compiler_params=ROOM,
         cost_estimate=cost(10**5, 5 * 10**5),
         name="depth",
     )(deep, low)
@@ -354,6 +355,7 @@
         in_specs=[VMEM] * 4,
         out_specs=VMEM,
         scratch_shapes=[pltpu.VMEM((LEVELS * PROBES, 2 * RANK), F32)],
+        compiler_params=ROOM,
         cost_estimate=cost(10**9, 3 * 10**6),
         name="final",
     )(wide, factor, coupling, diagonal)

time: 101 us -> 88 us (0.87)
  Pallas kernels: 20.4 us -> 9.59 us
  blocking collectives: 55.1 us -> 51.7 us
  starting transfers between devices: 23.3 us -> 21 us
  local copies, waits for them, and re-layouts: 1.25 us -> 3.5 us
    all_to_all x3, blocking collectives: 55.1 us -> 51.7 us  [exchange(): return lax.all_to_all(value, axes, 0, 0, tiled=True)]
    pallas_call x1, Pallas kernels: 6.64 us -> 4.05 us  [on_device(): pl.pallas_call(near_kernel, out_shape=(jax.ShapeDtypeStruct((2, PROBES, L...]
    ppermute x3, starting transfers between devices: 23.3 us -> 21 us  [swap(): return lax.ppermute(value, axis, [(0, 1), (1, 0)])]
    unnamed x6 -> x12, local copies, waits for them, and re-layouts: 1.25 us -> 3.5 us
    pallas_call x1, Pallas kernels: 1.85 us -> 0.04 us  [on_device(): pl.pallas_call(depth_kernel, out_shape=jax.ShapeDtypeStruct((8, PROBES +...]
    pallas_call x1, Pallas kernels: 3.45 us -> 1.75 us  [on_device(): pl.pallas_call(final_kernel, out_shape=jax.ShapeDtypeStruct((2, PROBES, W...]
    pallas_call x1, Pallas kernels: 1.69 us -> 0.02 us  [on_device(): pl.pallas_call(plane_kernel, out_shape=jax.ShapeDtypeStruct((8, 3 * QUART...]
    pallas_call x1, Pallas kernels: 1.57 us -> 0.01 us  [on_device(): pl.pallas_call(prepare_kernel, out_shape=jax.ShapeDtypeStruct((TRANSFER,...]
  transfers between devices with their start and end apart: 3 -> 3, of which waited for: 0 -> 1; matrix products, arithmetic and copies ran while one was open for 0% -> 0% of each run, Pallas kernels for 7% -> 5%
where the time goes in v2:
time: 88 us; the launch traced here: 87.6 us
  blocking collectives  51.7 us (59%)
  starting transfers between devices  21 us (24%)
  Pallas kernels  9.59 us (11%)
  local copies, waits for them, and re-layouts  3.5 us (4%)
  waiting for transfers between devices  0.97 us (1%)
    all_to_all x3, blocking collectives, exchange(): return lax.all_to_all(value, axes, 0, 0, tiled=True)  51.7 us
    ppermute x3, starting transfers between devices, swap(): return lax.ppermute(value, axis, [(0, 1), (1, 0)])  21 us
    pallas_call x1, Pallas kernels, on_device(): pl.pallas_call(near_kernel, out_shape=(jax.ShapeDtypeStruct((2, PROBES, L...  4.05 us
    pallas_call x1, Pallas kernels, on_device(): pl.pallas_call(far_kernel, out_shape=(jax.ShapeDtypeStruct((2, PROBES, WI...  3.72 us
    unnamed x12, local copies, waits for them, and re-layouts  3.5 us
  transfers between devices with their start and end apart: 3, of which 1 were waited for; matrix products, arithmetic and copies ran while one was open for 0% of the time, Pallas kernels for 5%

profile of v2, /device:TPU:1, one launch (start us, length us, event | category | flops | bytes accessed | tf_op | source)
XLA Modules:
  0.0 87.6 jit_solution(14468847792579503326)
XLA Ops:
  0.0 0.0 copy-start
  0.0 0.9 %copy-done = f32[64,512]{1,0:T(8,128)S(1)} copy-done((f32[64,512]{1,0:T(8,128)S(1)}, f32[64,512]{1,0:T(8,128)}, u32[]{:S(2)}) %copy-start) | copy-done | bytes 131096
  0.9 0.0 copy-start.1
  0.9 0.7 copy-done.1
  1.6 8.7 %collective-permute-start.1 = (bf16[80,512]{1,0:T(8,128)(2,1)S(1)}, bf16[80,512]{1,0:T(8,128)(2,1)S(1)}, u32[]{:S(2)}, u32[]{:S(2)}) collective-permute-start(bf16[80,512]{1,0:T(8,128)(2,1)S(1)} %prepare.1.own_ref), channel_id=1, source_target_pairs={{0,1},{1,0},{2,3},{3,2},{4,5},{5,4},{6,7},{7,6},{8,9},{9,8},{10,11... | collective-permute-start | bytes 245768 | tf_op jit(solution)/shard_map/ppermute | solution.py:283
  10.4 10.1 %collective-permute-start = (bf16[80,512]{1,0:T(8,128)(2,1)S(1)}, bf16[80,512]{1,0:T(8,128)(2,1)S(1)}, u32[]{:S(2)}, u32[]{:S(2)}) collective-permute-start(bf16[80,512]{1,0:T(8,128)(2,1)S(1)} %prepare.1.own_ref), channel_id=1, source_target_pairs={{0,2},{2,0},{1,3},{3,1},{4,6},{6,4},{5,7},{7,5},{8,10},{10,8},{9,1... | collective-permute-start | bytes 245768 | tf_op jit(solution)/shard_map/ppermute | solution.py:283
  21.1 0.0 collective-permute-done.1.other_ref
  21.2 0.0 copy-start.2
  21.2 1.2 %copy-done.2 = f32[254,8,128]{2,1,0:T(8,128)S(1)} copy-done((f32[254,8,128]{2,1,0:T(8,128)S(1)}, f32[254,8,128]{2,1,0:T(8,128)}, u32[]{:S(2)}) %copy-start.2) | copy-done | bytes 1040408
  22.4 0.0 copy-start.4
  22.4 0.7 copy-done.4
  23.0 0.0 copy-start.5
  23.0 4.1 %near.1 = (f32[2,64,1024]{2,1,0:T(8,128)S(1)}, bf16[128,1024]{1,0:T(8,128)(2,1)S(1)}, bf16[2,896,512]{2,1,0:T(8,128)(2,1)S(1)}) custom-call(bf16[80,512]{1,0:T(8,128)(2,1)S(1)} %prepare.1.own_ref, bf16[80,512]{1,0:T(8,128)(2,1)S(1)} %collective-permute-done.1.other_ref, f32[8]{0:T(128)S(1)} %copy-done.4, f32[1]{0:T(128)S(6)} %copy.7.strength_ref, ...), custom_call_target="tpu_custom_call" | custom-call | flops 2000000000 | bytes 3000000 | tf_op jit(solution)/shard_map/near/pallas_call | solution.py:302
  27.1 0.0 collective-permute-done.far_ref
  27.1 2.2 %collective-permute-start.2 = (bf16[80,512]{1,0:T(8,128)(2,1)S(1)}, bf16[80,512]{1,0:T(8,128)(2,1)S(1)}, u32[]{:S(2)}, u32[]{:S(2)}) collective-permute-start(bf16[80,512]{1,0:T(8,128)(2,1)S(1)} %collective-permute-done.far_ref), channel_id=1, source_target_pairs={{0,1},{1,0},{2,3},{3,2},{4,5},{5,4},{6,7},{7,6},{8,9},{9,8},{10,11... | collective-permute-start | bytes 245768 | tf_op jit(solution)/shard_map/ppermute | solution.py:283
  29.3 1.0 %collective-permute-done.2.cross_ref = bf16[80,512]{1,0:T(8,128)(2,1)S(1)} collective-permute-done((bf16[80,512]{1,0:T(8,128)(2,1)S(1)}, bf16[80,512]{1,0:T(8,128)(2,1)S(1)}, u32[]{:S(2)}, u32[]{:S(2)}) %collective-permute-start.2) | collective-permute-done | bytes 81952 | tf_op jit(solution)/shard_map/ppermute | solution.py:283
  30.3 0.0 copy-done.5
  30.3 3.7 %far.1 = (f32[2,64,512]{2,1,0:T(8,128)S(1)}, f32[16,48,128]{2,1,0:T(8,128)S(1)}, f32[4,64,128]{2,1,0:T(8,128)S(1)}) custom-call(bf16[80,512]{1,0:T(8,128)(2,1)S(1)} %collective-permute-done.far_ref, bf16[80,512]{1,0:T(8,128)(2,1)S(1)} %collective-permute-done.2.cross_ref, f32[8]{0:T(128)S(1)} %copy-done.5, f32[1]{0:T(128)S(6)} %copy.7.strength_ref, ...), custom_call_target="tpu_custom_call" | custom-call | flops 1000000000 | bytes 2000000 | tf_op jit(solution)/shard_map/far/pallas_call | solution.py:317
  34.0 0.0 copy-start.3
  34.0 16.0 %all_to_all.15.got_ref = f32[16,48,128]{2,1,0:T(8,128)S(1)} all-to-all(f32[16,48,128]{2,1,0:T(8,128)S(1)} %get-tuple-element.19), channel_id=1, replica_groups=mesh['x'=4,'z'=8,'y'=4,'h'=2,'c'=2] {'x','y'}, dimensions={0} | all-to-all | bytes 786432 | tf_op jit(solution)/shard_map/all_to_all | solution.py:287
  50.0 19.2 %all_to_all.16.got_ref = f32[8,48,128]{2,1,0:T(8,128)S(1)} all-to-all(f32[8,48,128]{2,1,0:T(8,128)S(1)} %plane.1), channel_id=1, replica_groups=mesh['x'=4,'z'=8,'y'=4,'h'=2,'c'=2] {'z'}, dimensions={0} | all-to-all | bytes 393216 | tf_op jit(solution)/shard_map/all_to_all | solution.py:287
  69.2 16.6 %all_to_all.17.got_ref = f32[8,144,128]{2,1,0:T(8,128)S(1)} all-to-all(f32[8,144,128]{2,1,0:T(8,128)S(1)} %depth.1), channel_id=1, replica_groups=mesh['x'=4,'z'=8,'y'=4,'h'=2,'c'=2] {'y','c'}, dimensions={0} | all-to-all | bytes 1179648 | tf_op jit(solution)/shard_map/all_to_all | solution.py:287
  85.8 0.0 copy-done.3
  85.8 1.7 %final.1 = f32[2,64,512]{2,1,0:T(8,128)} custom-call(f32[8,144,128]{2,1,0:T(8,128)S(1)} %all_to_all.17.got_ref, bf16[2,896,512]{2,1,0:T(8,128)(2,1)S(1)} %get-tuple-element.21.factor_ref, f32[128,128]{1,0:T(8,128)S(1)} %copy-done.3, f32[2,64,512]{2,1,0:T(8,128)S(1)} %get-tuple-element.22.diagonal_ref), custom_call_target="tpu_custom_call" | custom-call | flops 1000000000 | bytes 3000000 | tf_op jit(solution)/shard_map/final/pallas_call | solution.py:352
  (3 shorter events, 0.1 us)
Async XLA Ops:
  0.0 0.9 %copy-start = (f32[64,512]{1,0:T(8,128)S(1)}, f32[64,512]{1,0:T(8,128)}, u32[]{:S(2)}) copy-start(f32[64,512]{1,0:T(8,128)} %probes_ref.1) | copy-start | bytes 393220
  0.9 0.7 copy-start.1
  1.6 19.5 %collective-permute-start.1 = (bf16[80,512]{1,0:T(8,128)(2,1)S(1)}, bf16[80,512]{1,0:T(8,128)(2,1)S(1)}, u32[]{:S(2)}, u32[]{:S(2)}) collective-permute-start(bf16[80,512]{1,0:T(8,128)(2,1)S(1)} %prepare.1.own_ref), channel_id=1, source_target_pairs={{0,1},{1,0},{2,3},{3,2},{4,5},{5,4},{6,7},{7,6},{8,9},{9,8},{10,11... | collective-permute-start | bytes 245768 | tf_op jit(solution)/shard_map/ppermute | solution.py:283
  10.4 16.7 %collective-permute-start = (bf16[80,512]{1,0:T(8,128)(2,1)S(1)}, bf16[80,512]{1,0:T(8,128)(2,1)S(1)}, u32[]{:S(2)}, u32[]{:S(2)}) collective-permute-start(bf16[80,512]{1,0:T(8,128)(2,1)S(1)} %prepare.1.own_ref), channel_id=1, source_target_pairs={{0,2},{2,0},{1,3},{3,1},{4,6},{6,4},{5,7},{7,5},{8,10},{10,8},{9,1... | collective-permute-start | bytes 245768 | tf_op jit(solution)/shard_map/ppermute | solution.py:283
  21.2 1.2 %copy-start.2 = (f32[254,8,128]{2,1,0:T(8,128)S(1)}, f32[254,8,128]{2,1,0:T(8,128)}, u32[]{:S(2)}) copy-start(f32[254,8,128]{2,1,0:T(8,128)} %marks_ref.1) | copy-start | bytes 3121156
  22.4 0.7 copy-start.4
  23.0 7.2 %copy-start.5 = (f32[8]{0:T(128)S(1)}, f32[8]{0:T(128)}, u32[]{:S(2)}) copy-start(f32[8]{0:T(128)} %scales_ref.3) | copy-start | bytes 100
  27.1 3.2 %collective-permute-start.2 = (bf16[80,512]{1,0:T(8,128)(2,1)S(1)}, bf16[80,512]{1,0:T(8,128)(2,1)S(1)}, u32[]{:S(2)}, u32[]{:S(2)}) collective-permute-start(bf16[80,512]{1,0:T(8,128)(2,1)S(1)} %collective-permute-done.far_ref), channel_id=1, source_target_pairs={{0,1},{1,0},{2,3},{3,2},{4,5},{5,4},{6,7},{7,6},{8,9},{9,8},{10,11... | collective-permute-start | bytes 245768 | tf_op jit(solution)/shard_map/ppermute | solution.py:283
  34.0 51.8 %copy-start.3 = (f32[128,128]{1,0:T(8,128)S(1)}, f32[128,128]{1,0:T(8,128)}, u32[]{:S(2)}) copy-start(f32[128,128]{1,0:T(8,128)} %coupling_ref.1) | copy-start | bytes 196612

commit v3 on v2

--- a/solution.py
+++ b/solution.py
@@ -22,6 +22,9 @@
 TWO_LN2 = 2.0 * math.log(2.0)
 F32 = jnp.float32
 BF16 = jnp.bfloat16
+I16 = jnp.int16
+FINE = 2.0**26
+OCTAVES = 44.0
 VMEM = pl.BlockSpec(memory_space=pltpu.VMEM)
 ROOM = pltpu.CompilerParams(vmem_limit_bytes=16 * 2**20)
 SMEM = pl.BlockSpec(memory_space=pltpu.SMEM)
@@ -37,14 +40,6 @@
     second = rest.astype(BF16).astype(F32)
     third = (rest - second).astype(BF16).astype(F32)
     return first, second, third
-
-
-def inverse_scales(scales_ref):
-    row = lax.broadcasted_iota(jnp.int32, (8, 128), 0)
-    held = jnp.full((8, 128), scales_ref[0], F32)
-    for k in range(1, 8):
-        held = jnp.where(row == k, scales_ref[k], held)
-    return (ROOT / held)[:, :1]
 
 
 def norms(value):
@@ -89,17 +84,46 @@
     return top, (value - top.astype(F32)).astype(BF16)
 
 
-def log2_strength(strength_ref):
-    return jnp.log(jnp.full((1, 128), strength_ref[0], F32))[:, :1] * math.log2(math.e)
-
-
-def prepare_kernel(coords_ref, probes_ref, out_ref):
-    coords = coords_ref[...]
+def encode(value):
+    grade = jnp.log(1.0 + jnp.abs(value) * FINE) * (32767.0 / (OCTAVES * math.log(2.0))) + 0.5
+    return jnp.where(value < 0.0, -grade, grade).astype(jnp.int32).astype(jnp.int16)
+
+
+def decode(code):
+    grade = code.astype(jnp.int32).astype(F32)
+    size = (jnp.exp2(jnp.abs(grade) * (OCTAVES / 32767.0)) - 1.0) * (1.0 / FINE)
+    return jnp.where(grade < 0.0, -size, size)
+
+
+def prepare_kernel(
+    coords_ref, probes_ref, marks_ref, scales_ref, strength_ref,
+    out_ref, picked_ref, facts_ref, coords_buf, probes_buf, scales_buf, sem,
+):
+    row = lax.axis_index("x") * 32 + lax.axis_index("z") * 4 + lax.axis_index("y")
+    copies = [
+        pltpu.make_async_copy(probes_ref, probes_buf, sem.at[0]),
+        pltpu.make_async_copy(coords_ref, coords_buf, sem.at[1]),
+        pltpu.make_async_copy(scales_ref, scales_buf, sem.at[2 + LEVELS]),
+    ]
+    for level in range(LEVELS):
+        node = 2 ** (LEVELS - level) - 2 + jnp.right_shift(row, level)
+        copies.append(pltpu.make_async_copy(marks_ref.at[node], picked_ref.at[level], sem.at[2 + level]))
+    for copy in copies:
+        copy.start()
+    for copy in copies:
+        copy.wait()
+    coords = coords_buf[...]
     high = jnp.right_shift(coords, 6)
     low = coords - high * 64
-    out_ref[0:PROBES, :] = probes_ref[...].astype(BF16)
+    out_ref[0:PROBES, :] = probes_buf[...].astype(BF16)
     both = jnp.concatenate([high.astype(F32), low.astype(F32)], axis=0)
     out_ref[PROBES:TRANSFER, :] = both.astype(BF16)
+    place = lax.broadcasted_iota(jnp.int32, (8, 128), 0)
+    held = jnp.full((8, 128), scales_buf[0], F32)
+    for k in range(1, 8):
+        held = jnp.where(place == k, scales_buf[k], held)
+    facts_ref[0:8, :] = ROOT / held
+    facts_ref[8:16, :] = jnp.log(jnp.full((8, 128), strength_ref[0], F32)) * math.log2(math.e)
 
 
 def accumulate(message_ref, inverse, right, log_strength, held_k, held_s, fresh):
@@ -127,18 +151,14 @@
 
 
 def near_kernel(
-    own_ref, other_ref, scales_ref, strength_ref, marks_ref,
+    own_ref, other_ref, facts_ref, marks_ref,
     held_ref, right_ref, factor_ref,
 ):
-    row = lax.axis_index("x") * 32 + lax.axis_index("z") * 4 + lax.axis_index("y")
     core = lax.axis_index("c")
-    inverse = inverse_scales(scales_ref)
-    log_strength = log2_strength(strength_ref)
+    inverse = facts_ref[0:8, 0:1]
+    log_strength = facts_ref[8:9, 0:1]
     own = points_of(own_ref[...], inverse)
-    marks = []
-    for level in range(LEVELS):
-        node = 2 ** (LEVELS - level) - 2 + jnp.right_shift(row, level)
-        marks.append((marks_ref[node] - 0.5) * inverse)
+    marks = [(marks_ref[level] - 0.5) * inverse for level in range(LEVELS)]
     halves = [jnp.where(core == 0, mark[:, :HALF], mark[:, HALF:]) for mark in marks]
     halves.append(jnp.zeros((8, HALF), F32))
     columns = jnp.concatenate([own] + halves, axis=1)
@@ -156,13 +176,13 @@
 
 
 def far_kernel(
-    far_ref, cross_ref, scales_ref, strength_ref, held_ref, right_ref,
+    far_ref, cross_ref, facts_ref, held_ref, right_ref,
     diagonal_ref, plane_ref, low_ref, sums,
 ):
     x = lax.axis_index("x")
     y = lax.axis_index("y")
-    inverse = inverse_scales(scales_ref)
-    log_strength = log2_strength(strength_ref)
+    inverse = facts_ref[0:8, 0:1]
+    log_strength = facts_ref[8:9, 0:1]
     right = right_ref[...]
     sums[...] = held_ref[...]
     accumulate(far_ref, inverse, right, log_strength, sums.at[0], sums.at[1], False)
@@ -172,15 +192,15 @@
     for level in range(LEVELS):
         at = WIDTH + level * HALF
         pair = [sums[0, :, at : at + HALF], sums[1, :, at : at + HALF]]
-        units.append(jnp.concatenate(pair, axis=1))
-    blank = jnp.zeros((2 * QUARTER, 128), F32)
+        units.append(encode(jnp.concatenate(pair, axis=1)))
+    blank = jnp.zeros((2 * QUARTER, 128), I16)
     for at in range(4):
         part = slice(at * QUARTER, (at + 1) * QUARTER)
         mine = jnp.concatenate([units[2][part], units[3][part], units[4][part]], axis=0)
         plane_ref[x * 4 + at] = mine
         for apart, level in ((1, 5), (2, 6), (3, 6)):
             plane_ref[jnp.bitwise_xor(x, apart) * 4 + at] = jnp.concatenate([units[level][part], blank], axis=0)
-    low_ref[y] = jnp.zeros((PROBES, 128), F32)
+    low_ref[y] = jnp.zeros((PROBES, 128), I16)
     for apart, level in ((1, 0), (2, 1), (3, 1)):
         low_ref[jnp.bitwise_xor(y, apart)] = units[level]
 
@@ -191,14 +211,14 @@
 
     def total(apart, rows):
         start = jnp.bitwise_xor(x, apart) * 4
-        parts = [got_ref[start + at, rows] for at in range(4)]
+        parts = [decode(got_ref[start + at, rows]) for at in range(4)]
         return (parts[0] + parts[1]) + (parts[2] + parts[3])
 
     low, middle, high = slice(0, 16), slice(16, 32), slice(32, 48)
     sums = [total(0, low), total(0, middle), total(0, high)]
-    five = total(1, low)
-    six = total(2, low) + total(3, low)
-    chosen = [jnp.zeros((QUARTER, 128), F32)] + sums
+    five = encode(total(1, low))
+    six = encode(total(2, low) + total(3, low))
+    chosen = [jnp.zeros((QUARTER, 128), I16)] + [encode(value) for value in sums]
     for apart in range(8):
         which = apart.bit_length()
         out_ref[jnp.bitwise_xor(z, apart)] = jnp.concatenate([chosen[which], five, six], axis=0)
@@ -208,7 +228,7 @@
     z = lax.axis_index("z")
 
     def piece(apart, start):
-        return got_ref[jnp.bitwise_xor(z, apart), start : start + QUARTER]
+        return decode(got_ref[jnp.bitwise_xor(z, apart), start : start + QUARTER])
 
     two = piece(1, 0)
     three = piece(2, 0) + piece(3, 0)
@@ -219,7 +239,7 @@
         while len(parts) > 1:
             parts = [a + b for a, b in zip(parts[::2], parts[1::2])]
         found.append(parts[0])
-    packed = jnp.concatenate(found, axis=0)
+    packed = jnp.concatenate([encode(value) for value in found], axis=0)
     for at in range(4):
         for core in range(2):
             out_ref[2 * at + core, 0:PROBES] = low_ref[at]
@@ -231,15 +251,15 @@
     row = lax.axis_index("x") * 32 + lax.axis_index("z") * 4 + y
     for core in range(2):
         lanes = slice(core * 128, core * 128 + 128)
-        sibling[0:PROBES, lanes] = got_ref[jnp.bitwise_xor(y, 1) * 2 + core, 0:PROBES]
-        pair = got_ref[jnp.bitwise_xor(y, 2) * 2 + core, 0:PROBES]
-        pair = pair + got_ref[jnp.bitwise_xor(y, 3) * 2 + core, 0:PROBES]
+        sibling[0:PROBES, lanes] = decode(got_ref[jnp.bitwise_xor(y, 1) * 2 + core, 0:PROBES])
+        pair = decode(got_ref[jnp.bitwise_xor(y, 2) * 2 + core, 0:PROBES])
+        pair = pair + decode(got_ref[jnp.bitwise_xor(y, 3) * 2 + core, 0:PROBES])
         sibling[PROBES : 2 * PROBES, lanes] = pair
         for level in range(2, LEVELS):
             for at in range(4):
                 start = level * PROBES + at * QUARTER
                 source = PROBES + (level - 2) * QUARTER
-                sibling[start : start + QUARTER, lanes] = got_ref[2 * at + core, source : source + QUARTER]
+                sibling[start : start + QUARTER, lanes] = decode(got_ref[2 * at + core, source : source + QUARTER])
     coupling = coupling_ref[...]
     blank = jnp.zeros((HALF, RANK), F32)
 
@@ -279,6 +299,10 @@
     out_ref[1] = diagonal_ref[1] + (on_kern[PROBES:] + on_slope)
 
 
+def stay(array):
+    return pltpu.with_memory_space_constraint(array, pltpu.HBM)
+
+
 def swap(value, axis):
     return lax.ppermute(value, axis, [(0, 1), (1, 0)])
 
@@ -288,15 +312,25 @@
 
 
 def on_device(coords, probes, lengthscales, amplitude, landmarks, coupling):
-    message = pl.pallas_call(
+    message, marks, facts = pl.pallas_call(
         prepare_kernel,
-        out_shape=jax.ShapeDtypeStruct((TRANSFER, WIDTH), BF16),
-        in_specs=[VMEM, VMEM],
-        out_specs=VMEM,
+        out_shape=(
+            jax.ShapeDtypeStruct((TRANSFER, WIDTH), BF16),
+            jax.ShapeDtypeStruct((LEVELS, 8, RANK), F32),
+            jax.ShapeDtypeStruct((16, 128), F32),
+        ),
+        in_specs=[pl.BlockSpec(memory_space=pltpu.HBM)] * 4 + [SMEM],
+        out_specs=(VMEM, VMEM, VMEM),
+        scratch_shapes=[
+            pltpu.VMEM((8, WIDTH), jnp.int32),
+            pltpu.VMEM((PROBES, WIDTH), F32),
+            pltpu.SMEM((8,), F32),
+            pltpu.SemaphoreType.DMA((3 + LEVELS,)),
+        ],
         compiler_params=ROOM,
         cost_estimate=cost(10**5, 2 * 10**5),
         name="prepare",
-    )(coords, probes)
+    )(*[stay(array) for array in (coords, probes, landmarks, lengthscales)], amplitude)
     far = swap(message, "h")
     other = swap(message, "c")
     held, right, factor = pl.pallas_call(
@@ -306,32 +340,32 @@
             jax.ShapeDtypeStruct((SPAN, LANES), BF16),
             jax.ShapeDtypeStruct((2, LEVELS * RANK, WIDTH), BF16),
         ),
-        in_specs=[VMEM, VMEM, SMEM, SMEM, VMEM],
+        in_specs=[VMEM] * 4,
         out_specs=(VMEM, VMEM, VMEM),
         compiler_params=ROOM,
         cost_estimate=cost(2 * 10**9, 3 * 10**6),
         name="near",
-    )(message, other, lengthscales, amplitude, landmarks)
+    )(message, other, facts, marks)
     far, held, right = lax.optimization_barrier((far, held, right))
     cross = swap(far, "c")
     diagonal, plane, low = pl.pallas_call(
         far_kernel,
         out_shape=(
             jax.ShapeDtypeStruct((2, PROBES, WIDTH), F32),
-            jax.ShapeDtypeStruct((16, 3 * QUARTER, 128), F32),
-            jax.ShapeDtypeStruct((4, PROBES, 128), F32),
+            jax.ShapeDtypeStruct((16, 3 * QUARTER, 128), I16),
+            jax.ShapeDtypeStruct((4, PROBES, 128), I16),
         ),
-        in_specs=[VMEM, VMEM, SMEM, SMEM, VMEM, VMEM],
+        in_specs=[VMEM] * 5,
         out_specs=(VMEM, VMEM, VMEM),
         scratch_shapes=[pltpu.VMEM((2, PROBES, LANES), F32)],
         compiler_params=ROOM,
         cost_estimate=cost(10**9, 2 * 10**6),
         name="far",
-    )(far, cross, lengthscales, amplitude, held, right)
+    )(far, cross, facts, held, right)
     plane = exchange(plane, ("x", "y"))
     deep = pl.pallas_call(
         plane_kernel,
-        out_shape=jax.ShapeDtypeStruct((8, 3 * QUARTER, 128), F32),
+        out_shape=jax.ShapeDtypeStruct((8, 3 * QUARTER, 128), I16),
         in_specs=[VMEM],
         out_specs=VMEM,
         compiler_params=ROOM,
@@ -341,7 +375,7 @@
     deep = exchange(deep, "z")
     wide = pl.pallas_call(
         depth_kernel,
-        out_shape=jax.ShapeDtypeStruct((8, PROBES + 5 * QUARTER, 128), F32),
+        out_shape=jax.ShapeDtypeStruct((8, PROBES + 5 * QUARTER, 128), I16),
         in_specs=[VMEM, VMEM],
         out_specs=VMEM,
         compiler_params=ROOM,

time: 88 us -> 81 us (0.920)
  blocking collectives: 51.7 us -> 46.6 us
  local copies, waits for them, and re-layouts: 3.5 us -> 0.01 us
  waiting for transfers between devices: 0.97 us -> 1.93 us
    all_to_all x3, blocking collectives: 51.7 us -> 46.6 us  [exchange(): return lax.all_to_all(value, axes, 0, 0, tiled=True)]
    unnamed x12 -> x2, local copies, waits for them, and re-layouts: 3.5 us -> 0.01 us
    pallas_call x1, Pallas kernels: 0.01 us -> 1.03 us  [on_device(): pl.pallas_call(prepare_kernel, out_shape=(jax.ShapeDtypeStruct((TRANSFER,...]
    ppermute x3, waiting for transfers between devices: 0.97 us -> 1.93 us  [swap(): return lax.ppermute(value, axis, [(0, 1), (1, 0)])]
  transfers between devices with their start and end apart: 3 -> 3, of which waited for: 1 -> 2; matrix products, arithmetic and copies ran while one was open for 0% -> 0% of each run, Pallas kernels for 5% -> 4%
where the time goes in v3:
time: 81 us; the launch traced here: 80.6 us
  blocking collectives  46.6 us (58%)
  starting transfers between devices  21.7 us (27%)
  Pallas kernels  9.72 us (12%)
  waiting for transfers between devices  1.93 us (2%)
    all_to_all x3, blocking collectives, exchange(): return lax.all_to_all(value, axes, 0, 0, tiled=True)  46.6 us
    ppermute x3, starting transfers between devices, swap(): return lax.ppermute(value, axis, [(0, 1), (1, 0)])  21.7 us
    pallas_call x1, Pallas kernels, on_device(): pl.pallas_call(near_kernel, out_shape=(jax.ShapeDtypeStruct((2, PROBES, L...  3.44 us
    pallas_call x1, Pallas kernels, on_device(): pl.pallas_call(far_kernel, out_shape=(jax.ShapeDtypeStruct((2, PROBES, WI...  3.24 us
    ppermute x3, waiting for transfers between devices, swap(): return lax.ppermute(value, axis, [(0, 1), (1, 0)])  1.93 us
    pallas_call x1, Pallas kernels, on_device(): pl.pallas_call(final_kernel, out_shape=jax.ShapeDtypeStruct((2, PROBES, W...  1.78 us
  transfers between devices with their start and end apart: 3, of which 2 were waited for; matrix products, arithmetic and copies ran while one was open for 0% of the time, Pallas kernels for 4%

profile of v3, /device:TPU:1, one launch (start us, length us, event | category | flops | bytes accessed | tf_op | source)
XLA Modules:
  0.0 80.6 jit_solution(5317366165110215304)
XLA Ops:
  0.7 1.0 %prepare.1 = (bf16[80,512]{1,0:T(8,128)(2,1)S(1)}, f32[7,8,128]{2,1,0:T(8,128)S(1)}, f32[16,128]{1,0:T(8,128)S(1)}) custom-call(s32[8,512]{1,0:T(8,128)} %coords_ref.1, f32[64,512]{1,0:T(8,128)} %probes_ref.1, f32[254,8,128]{2,1,0:T(8,128)} %marks_ref.1, f32[8]{0:T(128)} %scales_ref.1, f32[1]{0:T(128)S(6)} %copy.7.strength_ref), custom_call_target="tpu_custom_call" | custom-call | flops 100000 | bytes 200000 | tf_op jit(solution)/shard_map/prepare/pallas_call | solution.py:315
  1.7 8.7 %collective-permute-start.1 = (bf16[80,512]{1,0:T(8,128)(2,1)S(1)}, bf16[80,512]{1,0:T(8,128)(2,1)S(1)}, u32[]{:S(2)}, u32[]{:S(2)}) collective-permute-start(bf16[80,512]{1,0:T(8,128)(2,1)S(1)} %get-tuple-element.17.own_ref), channel_id=1, source_target_pairs={{0,1},{1,0},{2,3},{3,2},{4,5},{5,4},{6,7},{7,6},{8,9},{9,8},{10,11... | collective-permute-start | bytes 245768 | tf_op jit(solution)/shard_map/ppermute | solution.py:307
  10.4 10.1 %collective-permute-start = (bf16[80,512]{1,0:T(8,128)(2,1)S(1)}, bf16[80,512]{1,0:T(8,128)(2,1)S(1)}, u32[]{:S(2)}, u32[]{:S(2)}) collective-permute-start(bf16[80,512]{1,0:T(8,128)(2,1)S(1)} %get-tuple-element.17.own_ref), channel_id=1, source_target_pairs={{0,2},{2,0},{1,3},{3,1},{4,6},{6,4},{5,7},{7,5},{8,10},{10,8},{9,1... | collective-permute-start | bytes 245768 | tf_op jit(solution)/shard_map/ppermute | solution.py:307
  20.5 0.0 collective-permute-done.1.other_ref
  20.6 3.4 %near.1 = (f32[2,64,1024]{2,1,0:T(8,128)S(1)}, bf16[128,1024]{1,0:T(8,128)(2,1)S(1)}, bf16[2,896,512]{2,1,0:T(8,128)(2,1)S(1)}) custom-call(bf16[80,512]{1,0:T(8,128)(2,1)S(1)} %get-tuple-element.17.own_ref, bf16[80,512]{1,0:T(8,128)(2,1)S(1)} %collective-permute-done.1.other_ref, f32[16,128]{1,0:T(8,128)S(1)} %get-tuple-element.18.facts_ref, ...), custom_call_target="tpu_custom_call" | custom-call | flops 2000000000 | bytes 3000000 | tf_op jit(solution)/shard_map/near/pallas_call | solution.py:336
  24.0 1.0 %collective-permute-done.far_ref = bf16[80,512]{1,0:T(8,128)(2,1)S(1)} collective-permute-done((bf16[80,512]{1,0:T(8,128)(2,1)S(1)}, bf16[80,512]{1,0:T(8,128)(2,1)S(1)}, u32[]{:S(2)}, u32[]{:S(2)}) %collective-permute-start) | collective-permute-done | bytes 81952 | tf_op jit(solution)/shard_map/ppermute | solution.py:307
  25.0 2.9 %collective-permute-start.2 = (bf16[80,512]{1,0:T(8,128)(2,1)S(1)}, bf16[80,512]{1,0:T(8,128)(2,1)S(1)}, u32[]{:S(2)}, u32[]{:S(2)}) collective-permute-start(bf16[80,512]{1,0:T(8,128)(2,1)S(1)} %collective-permute-done.far_ref), channel_id=1, source_target_pairs={{0,1},{1,0},{2,3},{3,2},{4,5},{5,4},{6,7},{7,6},{8,9},{9,8},{10,11... | collective-permute-start | bytes 245768 | tf_op jit(solution)/shard_map/ppermute | solution.py:307
  27.9 0.9 %collective-permute-done.2.cross_ref = bf16[80,512]{1,0:T(8,128)(2,1)S(1)} collective-permute-done((bf16[80,512]{1,0:T(8,128)(2,1)S(1)}, bf16[80,512]{1,0:T(8,128)(2,1)S(1)}, u32[]{:S(2)}, u32[]{:S(2)}) %collective-permute-start.2) | collective-permute-done | bytes 81952 | tf_op jit(solution)/shard_map/ppermute | solution.py:307
  28.8 3.2 %far.1 = (f32[2,64,512]{2,1,0:T(8,128)S(1)}, s16[16,48,128]{2,1,0:T(8,128)(2,1)S(1)}, s16[4,64,128]{2,1,0:T(8,128)(2,1)S(1)}) custom-call(bf16[80,512]{1,0:T(8,128)(2,1)S(1)} %collective-permute-done.far_ref, bf16[80,512]{1,0:T(8,128)(2,1)S(1)} %collective-permute-done.2.cross_ref, f32[16,128]{1,0:T(8,128)S(1)} %get-tuple-element.18.facts_ref, ...), custom_call_target="tpu_custom_call" | custom-call | flops 1000000000 | bytes 2000000 | tf_op jit(solution)/shard_map/far/pallas_call | solution.py:351
  32.0 0.0 copy-start
  32.1 12.1 %all_to_all.15.got_ref = s16[16,48,128]{2,1,0:T(8,128)(2,1)S(1)} all-to-all(s16[16,48,128]{2,1,0:T(8,128)(2,1)S(1)} %get-tuple-element.25), channel_id=1, replica_groups=mesh['x'=4,'z'=8,'y'=4,'h'=2,'c'=2] {'x','y'}, dimensions={0} | all-to-all | bytes 393216 | tf_op jit(solution)/shard_map/all_to_all | solution.py:311
  44.1 0.1 plane.1
  44.3 21.4 %all_to_all.16.got_ref = s16[8,48,128]{2,1,0:T(8,128)(2,1)S(1)} all-to-all(s16[8,48,128]{2,1,0:T(8,128)(2,1)S(1)} %plane.1), channel_id=1, replica_groups=mesh['x'=4,'z'=8,'y'=4,'h'=2,'c'=2] {'z'}, dimensions={0} | all-to-all | bytes 196608 | tf_op jit(solution)/shard_map/all_to_all | solution.py:311
  65.7 0.1 depth.1
  65.8 13.1 %all_to_all.17.got_ref = s16[8,144,128]{2,1,0:T(8,128)(2,1)S(1)} all-to-all(s16[8,144,128]{2,1,0:T(8,128)(2,1)S(1)} %depth.1), channel_id=1, replica_groups=mesh['x'=4,'z'=8,'y'=4,'h'=2,'c'=2] {'y','c'}, dimensions={0} | all-to-all | bytes 589824 | tf_op jit(solution)/shard_map/all_to_all | solution.py:311
  78.9 0.0 copy-done
  78.9 1.8 %final.1 = f32[2,64,512]{2,1,0:T(8,128)} custom-call(s16[8,144,128]{2,1,0:T(8,128)(2,1)S(1)} %all_to_all.17.got_ref, bf16[2,896,512]{2,1,0:T(8,128)(2,1)S(1)} %get-tuple-element.27.factor_ref, f32[128,128]{1,0:T(8,128)S(1)} %copy-done, f32[2,64,512]{2,1,0:T(8,128)S(1)} %get-tuple-element.28.diagonal_ref), custom_call_target="tpu_custom_call" | custom-call | flops 1000000000 | bytes 3000000 | tf_op jit(solution)/shard_map/final/pallas_call | solution.py:386
Async XLA Ops:
  1.7 18.9 %collective-permute-start.1 = (bf16[80,512]{1,0:T(8,128)(2,1)S(1)}, bf16[80,512]{1,0:T(8,128)(2,1)S(1)}, u32[]{:S(2)}, u32[]{:S(2)}) collective-permute-start(bf16[80,512]{1,0:T(8,128)(2,1)S(1)} %get-tuple-element.17.own_ref), channel_id=1, source_target_pairs={{0,1},{1,0},{2,3},{3,2},{4,5},{5,4},{6,7},{7,6},{8,9},{9,8},{10,11... | collective-permute-start | bytes 245768 | tf_op jit(solution)/shard_map/ppermute | solution.py:307
  10.4 14.6 %collective-permute-start = (bf16[80,512]{1,0:T(8,128)(2,1)S(1)}, bf16[80,512]{1,0:T(8,128)(2,1)S(1)}, u32[]{:S(2)}, u32[]{:S(2)}) collective-permute-start(bf16[80,512]{1,0:T(8,128)(2,1)S(1)} %get-tuple-element.17.own_ref), channel_id=1, source_target_pairs={{0,2},{2,0},{1,3},{3,1},{4,6},{6,4},{5,7},{7,5},{8,10},{10,8},{9,1... | collective-permute-start | bytes 245768 | tf_op jit(solution)/shard_map/ppermute | solution.py:307
  25.0 3.8 %collective-permute-start.2 = (bf16[80,512]{1,0:T(8,128)(2,1)S(1)}, bf16[80,512]{1,0:T(8,128)(2,1)S(1)}, u32[]{:S(2)}, u32[]{:S(2)}) collective-permute-start(bf16[80,512]{1,0:T(8,128)(2,1)S(1)} %collective-permute-done.far_ref), channel_id=1, source_target_pairs={{0,1},{1,0},{2,3},{3,2},{4,5},{5,4},{6,7},{7,6},{8,9},{9,8},{10,11... | collective-permute-start | bytes 245768 | tf_op jit(solution)/shard_map/ppermute | solution.py:307
  32.0 46.8 %copy-start = (f32[128,128]{1,0:T(8,128)S(1)}, f32[128,128]{1,0:T(8,128)}, u32[]{:S(2)}) copy-start(f32[128,128]{1,0:T(8,128)} %coupling_ref.1) | copy-start | bytes 196612

commit v4 on v3

--- a/solution.py
+++ b/solution.py
@@ -177,9 +177,8 @@
 
 def far_kernel(
     far_ref, cross_ref, facts_ref, held_ref, right_ref,
-    diagonal_ref, plane_ref, low_ref, sums,
+    diagonal_ref, line_ref, low_ref, sums,
 ):
-    x = lax.axis_index("x")
     y = lax.axis_index("y")
     inverse = facts_ref[0:8, 0:1]
     log_strength = facts_ref[8:9, 0:1]
@@ -193,53 +192,55 @@
         at = WIDTH + level * HALF
         pair = [sums[0, :, at : at + HALF], sums[1, :, at : at + HALF]]
         units.append(encode(jnp.concatenate(pair, axis=1)))
-    blank = jnp.zeros((2 * QUARTER, 128), I16)
     for at in range(4):
         part = slice(at * QUARTER, (at + 1) * QUARTER)
-        mine = jnp.concatenate([units[2][part], units[3][part], units[4][part]], axis=0)
-        plane_ref[x * 4 + at] = mine
-        for apart, level in ((1, 5), (2, 6), (3, 6)):
-            plane_ref[jnp.bitwise_xor(x, apart) * 4 + at] = jnp.concatenate([units[level][part], blank], axis=0)
+        line_ref[at] = jnp.concatenate([units[level][part] for level in range(2, LEVELS)], axis=0)
     low_ref[y] = jnp.zeros((PROBES, 128), I16)
     for apart, level in ((1, 0), (2, 1), (3, 1)):
         low_ref[jnp.bitwise_xor(y, apart)] = units[level]
 
 
-def plane_kernel(got_ref, out_ref):
+def line_kernel(got_ref, out_ref):
     x = lax.axis_index("x")
     z = lax.axis_index("z")
-
-    def total(apart, rows):
-        start = jnp.bitwise_xor(x, apart) * 4
-        parts = [decode(got_ref[start + at, rows]) for at in range(4)]
-        return (parts[0] + parts[1]) + (parts[2] + parts[3])
-
-    low, middle, high = slice(0, 16), slice(16, 32), slice(32, 48)
-    sums = [total(0, low), total(0, middle), total(0, high)]
-    five = encode(total(1, low))
-    six = encode(total(2, low) + total(3, low))
-    chosen = [jnp.zeros((QUARTER, 128), I16)] + [encode(value) for value in sums]
-    for apart in range(8):
-        which = apart.bit_length()
-        out_ref[jnp.bitwise_xor(z, apart)] = jnp.concatenate([chosen[which], five, six], axis=0)
+    total = (decode(got_ref[0]) + decode(got_ref[1])) + (decode(got_ref[2]) + decode(got_ref[3]))
+    packed = encode(total)
+    parts = [packed[at * QUARTER : (at + 1) * QUARTER] for at in range(LEVELS - 2)]
+    for aside in range(4):
+        for apart in range(8):
+            place = jnp.bitwise_xor(x, aside) * 8 + jnp.bitwise_xor(z, apart)
+            if aside > 0:
+                out_ref[place] = parts[2 + aside.bit_length()]
+            elif apart > 0:
+                out_ref[place] = parts[apart.bit_length() - 1]
+            else:
+                out_ref[place] = jnp.zeros((QUARTER, 128), I16)
+
+
+def added(parts):
+    while len(parts) > 1:
+        parts = [a + b for a, b in zip(parts[::2], parts[1::2])]
+    return parts[0]
 
 
 def depth_kernel(got_ref, low_ref, out_ref):
+    x = lax.axis_index("x")
     z = lax.axis_index("z")
 
-    def piece(apart, start):
-        return decode(got_ref[jnp.bitwise_xor(z, apart), start : start + QUARTER])
-
-    two = piece(1, 0)
-    three = piece(2, 0) + piece(3, 0)
-    four = (piece(4, 0) + piece(5, 0)) + (piece(6, 0) + piece(7, 0))
-    found = [two, three, four]
-    for start in (QUARTER, 2 * QUARTER):
-        parts = [piece(apart, start) for apart in range(8)]
-        while len(parts) > 1:
-            parts = [a + b for a, b in zip(parts[::2], parts[1::2])]
-        found.append(parts[0])
-    packed = jnp.concatenate([encode(value) for value in found], axis=0)
+    def total(asides, aparts):
+        return added([
+            decode(got_ref[jnp.bitwise_xor(x, aside) * 8 + jnp.bitwise_xor(z, apart)])
+            for aside in asides for apart in aparts
+        ])
+
+    found = [
+        total((0,), (1,)),
+        total((0,), (2, 3)),
+        total((0,), (4, 5, 6, 7)),
+        total((1,), range(8)),
+        total((2, 3), range(8)),
+    ]
+    packed = encode(jnp.concatenate(found, axis=0))
     for at in range(4):
         for core in range(2):
             out_ref[2 * at + core, 0:PROBES] = low_ref[at]
@@ -348,11 +349,11 @@
     )(message, other, facts, marks)
     far, held, right = lax.optimization_barrier((far, held, right))
     cross = swap(far, "c")
-    diagonal, plane, low = pl.pallas_call(
+    diagonal, line, low = pl.pallas_call(
         far_kernel,
         out_shape=(
             jax.ShapeDtypeStruct((2, PROBES, WIDTH), F32),
-            jax.ShapeDtypeStruct((16, 3 * QUARTER, 128), I16),
+            jax.ShapeDtypeStruct((4, 5 * QUARTER, 128), I16),
             jax.ShapeDtypeStruct((4, PROBES, 128), I16),
         ),
         in_specs=[VMEM] * 5,
@@ -362,17 +363,17 @@
         cost_estimate=cost(10**9, 2 * 10**6),
         name="far",
     )(far, cross, facts, held, right)
-    plane = exchange(plane, ("x", "y"))
+    line = exchange(line, "y")
     deep = pl.pallas_call(
-        plane_kernel,
-        out_shape=jax.ShapeDtypeStruct((8, 3 * QUARTER, 128), I16),
+        line_kernel,
+        out_shape=jax.ShapeDtypeStruct((32, QUARTER, 128), I16),
         in_specs=[VMEM],
         out_specs=VMEM,
         compiler_params=ROOM,
         cost_estimate=cost(10**5, 3 * 10**5),
-        name="plane",
-    )(plane)
-    deep = exchange(deep, "z")
+        name="line",
+    )(line)
+    deep = exchange(deep, ("x", "z"))
     wide = pl.pallas_call(
         depth_kernel,
         out_shape=jax.ShapeDtypeStruct((8, PROBES + 5 * QUARTER, 128), I16),

time: 81 us -> 81 us (level)
  no operation moved by 1% of the time
where the time goes in v4:
time: 81 us; the launch traced here: 80.6 us
  blocking collectives  46.4 us (57%)
  starting transfers between devices  21.8 us (27%)
  Pallas kernels  9.72 us (12%)
  waiting for transfers between devices  1.93 us (2%)
    all_to_all x3, blocking collectives, exchange(): return lax.all_to_all(value, axes, 0, 0, tiled=True)  46.4 us
    ppermute x3, starting transfers between devices, swap(): return lax.ppermute(value, axis, [(0, 1), (1, 0)])  21.8 us
    pallas_call x1, Pallas kernels, on_device(): pl.pallas_call(near_kernel, out_shape=(jax.ShapeDtypeStruct((2, PROBES, L...  3.44 us
    pallas_call x1, Pallas kernels, on_device(): pl.pallas_call(far_kernel, out_shape=(jax.ShapeDtypeStruct((2, PROBES, WI...  3.23 us
    ppermute x3, waiting for transfers between devices, swap(): return lax.ppermute(value, axis, [(0, 1), (1, 0)])  1.93 us
    pallas_call x1, Pallas kernels, on_device(): pl.pallas_call(final_kernel, out_shape=jax.ShapeDtypeStruct((2, PROBES, W...  1.78 us
  transfers between devices with their start and end apart: 3, of which 2 were waited for; matrix products, arithmetic and copies ran while one was open for 0% of the time, Pallas kernels for 4%

profile of v4, /device:TPU:1, one launch (start us, length us, event | category | flops | bytes accessed | tf_op | source)
XLA Modules:
  0.0 80.6 jit_solution(1975009489760484849)
XLA Ops:
  0.7 1.0 %prepare.1 = (bf16[80,512]{1,0:T(8,128)(2,1)S(1)}, f32[7,8,128]{2,1,0:T(8,128)S(1)}, f32[16,128]{1,0:T(8,128)S(1)}) custom-call(s32[8,512]{1,0:T(8,128)} %coords_ref.1, f32[64,512]{1,0:T(8,128)} %probes_ref.1, f32[254,8,128]{2,1,0:T(8,128)} %marks_ref.1, f32[8]{0:T(128)} %scales_ref.1, f32[1]{0:T(128)S(6)} %copy.7.strength_ref), custom_call_target="tpu_custom_call" | custom-call | flops 100000 | bytes 200000 | tf_op jit(solution)/shard_map/prepare/pallas_call | solution.py:316
  1.7 8.7 %collective-permute-start.1 = (bf16[80,512]{1,0:T(8,128)(2,1)S(1)}, bf16[80,512]{1,0:T(8,128)(2,1)S(1)}, u32[]{:S(2)}, u32[]{:S(2)}) collective-permute-start(bf16[80,512]{1,0:T(8,128)(2,1)S(1)} %get-tuple-element.17.own_ref), channel_id=1, source_target_pairs={{0,1},{1,0},{2,3},{3,2},{4,5},{5,4},{6,7},{7,6},{8,9},{9,8},{10,11... | collective-permute-start | bytes 245768 | tf_op jit(solution)/shard_map/ppermute | solution.py:308
  10.4 10.1 %collective-permute-start = (bf16[80,512]{1,0:T(8,128)(2,1)S(1)}, bf16[80,512]{1,0:T(8,128)(2,1)S(1)}, u32[]{:S(2)}, u32[]{:S(2)}) collective-permute-start(bf16[80,512]{1,0:T(8,128)(2,1)S(1)} %get-tuple-element.17.own_ref), channel_id=1, source_target_pairs={{0,2},{2,0},{1,3},{3,1},{4,6},{6,4},{5,7},{7,5},{8,10},{10,8},{9,1... | collective-permute-start | bytes 245768 | tf_op jit(solution)/shard_map/ppermute | solution.py:308
  20.5 0.0 collective-permute-done.1.other_ref
  20.6 3.4 %near.1 = (f32[2,64,1024]{2,1,0:T(8,128)S(1)}, bf16[128,1024]{1,0:T(8,128)(2,1)S(1)}, bf16[2,896,512]{2,1,0:T(8,128)(2,1)S(1)}) custom-call(bf16[80,512]{1,0:T(8,128)(2,1)S(1)} %get-tuple-element.17.own_ref, bf16[80,512]{1,0:T(8,128)(2,1)S(1)} %collective-permute-done.1.other_ref, f32[16,128]{1,0:T(8,128)S(1)} %get-tuple-element.18.facts_ref, ...), custom_call_target="tpu_custom_call" | custom-call | flops 2000000000 | bytes 3000000 | tf_op jit(solution)/shard_map/near/pallas_call | solution.py:337
  24.0 1.0 %collective-permute-done.far_ref = bf16[80,512]{1,0:T(8,128)(2,1)S(1)} collective-permute-done((bf16[80,512]{1,0:T(8,128)(2,1)S(1)}, bf16[80,512]{1,0:T(8,128)(2,1)S(1)}, u32[]{:S(2)}, u32[]{:S(2)}) %collective-permute-start) | collective-permute-done | bytes 81952 | tf_op jit(solution)/shard_map/ppermute | solution.py:308
  25.0 0.0 copy-start
  25.0 3.0 %collective-permute-start.2 = (bf16[80,512]{1,0:T(8,128)(2,1)S(1)}, bf16[80,512]{1,0:T(8,128)(2,1)S(1)}, u32[]{:S(2)}, u32[]{:S(2)}) collective-permute-start(bf16[80,512]{1,0:T(8,128)(2,1)S(1)} %collective-permute-done.far_ref), channel_id=1, source_target_pairs={{0,1},{1,0},{2,3},{3,2},{4,5},{5,4},{6,7},{7,6},{8,9},{9,8},{10,11... | collective-permute-start | bytes 245768 | tf_op jit(solution)/shard_map/ppermute | solution.py:308
  28.0 0.9 %collective-permute-done.2.cross_ref = bf16[80,512]{1,0:T(8,128)(2,1)S(1)} collective-permute-done((bf16[80,512]{1,0:T(8,128)(2,1)S(1)}, bf16[80,512]{1,0:T(8,128)(2,1)S(1)}, u32[]{:S(2)}, u32[]{:S(2)}) %collective-permute-start.2) | collective-permute-done | bytes 81952 | tf_op jit(solution)/shard_map/ppermute | solution.py:308
  28.9 3.2 %far.1 = (f32[2,64,512]{2,1,0:T(8,128)S(1)}, s16[4,80,128]{2,1,0:T(8,128)(2,1)S(1)}, s16[4,64,128]{2,1,0:T(8,128)(2,1)S(1)}) custom-call(bf16[80,512]{1,0:T(8,128)(2,1)S(1)} %collective-permute-done.far_ref, bf16[80,512]{1,0:T(8,128)(2,1)S(1)} %collective-permute-done.2.cross_ref, f32[16,128]{1,0:T(8,128)S(1)} %get-tuple-element.18.facts_ref, ...), custom_call_target="tpu_custom_call" | custom-call | flops 1000000000 | bytes 2000000 | tf_op jit(solution)/shard_map/far/pallas_call | solution.py:352
  32.2 7.0 %all_to_all.15.got_ref = s16[4,80,128]{2,1,0:T(8,128)(2,1)S(1)} all-to-all(s16[4,80,128]{2,1,0:T(8,128)(2,1)S(1)} %get-tuple-element.25), channel_id=1, replica_groups=mesh['x'=4,'z'=8,'y'=4,'h'=2,'c'=2] {'y'}, dimensions={0} | all-to-all | bytes 163840 | tf_op jit(solution)/shard_map/all_to_all | solution.py:312
  39.1 0.1 line.1
  39.2 26.0 %all_to_all.16.got_ref = s16[32,16,128]{2,1,0:T(8,128)(2,1)S(1)} all-to-all(s16[32,16,128]{2,1,0:T(8,128)(2,1)S(1)} %line.1), channel_id=1, replica_groups=mesh['x'=4,'z'=8,'y'=4,'h'=2,'c'=2] {'x','z'}, dimensions={0} | all-to-all | bytes 262144 | tf_op jit(solution)/shard_map/all_to_all | solution.py:312
  65.2 0.1 depth.1
  65.4 13.5 %all_to_all.17.got_ref = s16[8,144,128]{2,1,0:T(8,128)(2,1)S(1)} all-to-all(s16[8,144,128]{2,1,0:T(8,128)(2,1)S(1)} %depth.1), channel_id=1, replica_groups=mesh['x'=4,'z'=8,'y'=4,'h'=2,'c'=2] {'y','c'}, dimensions={0} | all-to-all | bytes 589824 | tf_op jit(solution)/shard_map/all_to_all | solution.py:312
  78.9 0.0 copy-done
  78.9 1.8 %final.1 = f32[2,64,512]{2,1,0:T(8,128)} custom-call(s16[8,144,128]{2,1,0:T(8,128)(2,1)S(1)} %all_to_all.17.got_ref, bf16[2,896,512]{2,1,0:T(8,128)(2,1)S(1)} %get-tuple-element.27.factor_ref, f32[128,128]{1,0:T(8,128)S(1)} %copy-done, f32[2,64,512]{2,1,0:T(8,128)S(1)} %get-tuple-element.28.diagonal_ref), custom_call_target="tpu_custom_call" | custom-call | flops 1000000000 | bytes 3000000 | tf_op jit(solution)/shard_map/final/pallas_call | solution.py:387
Async XLA Ops:
  1.7 18.9 %collective-permute-start.1 = (bf16[80,512]{1,0:T(8,128)(2,1)S(1)}, bf16[80,512]{1,0:T(8,128)(2,1)S(1)}, u32[]{:S(2)}, u32[]{:S(2)}) collective-permute-start(bf16[80,512]{1,0:T(8,128)(2,1)S(1)} %get-tuple-element.17.own_ref), channel_id=1, source_target_pairs={{0,1},{1,0},{2,3},{3,2},{4,5},{5,4},{6,7},{7,6},{8,9},{9,8},{10,11... | collective-permute-start | bytes 245768 | tf_op jit(solution)/shard_map/ppermute | solution.py:308
  10.4 14.6 %collective-permute-start = (bf16[80,512]{1,0:T(8,128)(2,1)S(1)}, bf16[80,512]{1,0:T(8,128)(2,1)S(1)}, u32[]{:S(2)}, u32[]{:S(2)}) collective-permute-start(bf16[80,512]{1,0:T(8,128)(2,1)S(1)} %get-tuple-element.17.own_ref), channel_id=1, source_target_pairs={{0,2},{2,0},{1,3},{3,1},{4,6},{6,4},{5,7},{7,5},{8,10},{10,8},{9,1... | collective-permute-start | bytes 245768 | tf_op jit(solution)/shard_map/ppermute | solution.py:308
  25.0 53.8 %copy-start = (f32[128,128]{1,0:T(8,128)S(1)}, f32[128,128]{1,0:T(8,128)}, u32[]{:S(2)}) copy-start(f32[128,128]{1,0:T(8,128)} %coupling_ref.1) | copy-start | bytes 196612
  25.0 3.9 %collective-permute-start.2 = (bf16[80,512]{1,0:T(8,128)(2,1)S(1)}, bf16[80,512]{1,0:T(8,128)(2,1)S(1)}, u32[]{:S(2)}, u32[]{:S(2)}) collective-permute-start(bf16[80,512]{1,0:T(8,128)(2,1)S(1)} %collective-permute-done.far_ref), channel_id=1, source_target_pairs={{0,1},{1,0},{2,3},{3,2},{4,5},{5,4},{6,7},{7,6},{8,9},{9,8},{10,11... | collective-permute-start | bytes 245768 | tf_op jit(solution)/shard_map/ppermute | solution.py:308

commit v5 on v3

--- a/solution.py
+++ b/solution.py
@@ -18,6 +18,9 @@
 TRANSFER = 80
 LANES = 1024
 BLOCK = 256
+KEPT = WIDTH + RANK
+ALL_SPANS = ((0, 256), (256, 512), (512, 768), (768, 1024))
+LATE_SPANS = ((0, 256), (256, 512), (512, 640))
 ROOT = math.sqrt(math.log2(math.e))
 TWO_LN2 = 2.0 * math.log(2.0)
 F32 = jnp.float32
@@ -126,34 +129,33 @@
     facts_ref[8:16, :] = jnp.log(jnp.full((8, 128), strength_ref[0], F32)) * math.log2(math.e)
 
 
-def accumulate(message_ref, inverse, right, log_strength, held_k, held_s, fresh):
+def accumulate(message_ref, facts_ref, right_ref, sums, spans, fresh):
     message = message_ref[...]
+    inverse = facts_ref[0:8, 0:1]
+    log_strength = facts_ref[8:9, 0:1]
     left = left_form(points_of(message, inverse), 0.0).T.astype(BF16)
     for block in range(WIDTH // BLOCK):
         rows = left[block * BLOCK : (block + 1) * BLOCK, :]
         signs = message[0:PROBES, block * BLOCK : (block + 1) * BLOCK]
-        for at in range(0, LANES, BLOCK):
-            exponent = jnp.dot(rows, right[:, at : at + BLOCK], preferred_element_type=F32)
-            sums = []
-            for value in kernel_pair(exponent, log_strength):
+        for start, stop in spans:
+            exponent = jnp.dot(rows, right_ref[:, start:stop], preferred_element_type=F32)
+            for which, value in enumerate(kernel_pair(exponent, log_strength)):
                 top, rest = halved(value)
                 total = jnp.dot(signs, top, preferred_element_type=F32)
-                if at >= WIDTH:
+                if start >= WIDTH:
                     total = total + jnp.dot(signs, rest, preferred_element_type=F32)
-                sums.append(total)
-            add_k, add_s = sums
-            if fresh and block == 0:
-                held_k[:, at : at + BLOCK] = add_k
-                held_s[:, at : at + BLOCK] = add_s
-            else:
-                held_k[:, at : at + BLOCK] += add_k
-                held_s[:, at : at + BLOCK] += add_s
-
-
-def near_kernel(
-    own_ref, other_ref, facts_ref, marks_ref,
-    held_ref, right_ref, factor_ref,
-):
+                if fresh and block == 0:
+                    sums[which, :, start:stop] = total
+                else:
+                    sums[which, :, start:stop] += total
+
+
+def unit_of(sums, level):
+    at = WIDTH + level * HALF
+    return encode(jnp.concatenate([sums[0, :, at : at + HALF], sums[1, :, at : at + HALF]], axis=1))
+
+
+def own_kernel(own_ref, facts_ref, marks_ref, held_ref, right_ref, factor_ref):
     core = lax.axis_index("c")
     inverse = facts_ref[0:8, 0:1]
     log_strength = facts_ref[8:9, 0:1]
@@ -162,11 +164,9 @@
     halves = [jnp.where(core == 0, mark[:, :HALF], mark[:, HALF:]) for mark in marks]
     halves.append(jnp.zeros((8, HALF), F32))
     columns = jnp.concatenate([own] + halves, axis=1)
-    right = right_form(columns, log_strength).astype(BF16)
-    right_ref[...] = right
-    accumulate(own_ref, inverse, right, log_strength, held_ref.at[0], held_ref.at[1], True)
-    accumulate(other_ref, inverse, right, log_strength, held_ref.at[0], held_ref.at[1], False)
-    own_right = right[:, :WIDTH]
+    right_ref[...] = right_form(columns, log_strength).astype(BF16)
+    accumulate(own_ref, facts_ref, right_ref, held_ref, ALL_SPANS, True)
+    own_right = right_ref[:, :WIDTH]
     for level in range(LEVELS):
         turned = left_form(marks[level], 0.0).T.astype(BF16)
         exponent = jnp.dot(turned, own_right, preferred_element_type=F32)
@@ -175,34 +175,18 @@
         factor_ref[1, level * RANK : (level + 1) * RANK, :] = slope.astype(BF16)
 
 
-def far_kernel(
-    far_ref, cross_ref, facts_ref, held_ref, right_ref,
-    diagonal_ref, plane_ref, low_ref, sums,
-):
+def near_kernel(other_ref, facts_ref, held_ref, right_ref, kept_ref, plane_ref, sums):
     x = lax.axis_index("x")
-    y = lax.axis_index("y")
-    inverse = facts_ref[0:8, 0:1]
-    log_strength = facts_ref[8:9, 0:1]
-    right = right_ref[...]
     sums[...] = held_ref[...]
-    accumulate(far_ref, inverse, right, log_strength, sums.at[0], sums.at[1], False)
-    accumulate(cross_ref, inverse, right, log_strength, sums.at[0], sums.at[1], False)
-    diagonal_ref[...] = sums[:, :, :WIDTH]
-    units = []
-    for level in range(LEVELS):
-        at = WIDTH + level * HALF
-        pair = [sums[0, :, at : at + HALF], sums[1, :, at : at + HALF]]
-        units.append(encode(jnp.concatenate(pair, axis=1)))
+    accumulate(other_ref, facts_ref, right_ref, sums, ALL_SPANS, False)
+    kept_ref[...] = sums[:, :, :KEPT]
+    units = [unit_of(sums, level) for level in range(2, LEVELS)]
     blank = jnp.zeros((2 * QUARTER, 128), I16)
     for at in range(4):
         part = slice(at * QUARTER, (at + 1) * QUARTER)
-        mine = jnp.concatenate([units[2][part], units[3][part], units[4][part]], axis=0)
-        plane_ref[x * 4 + at] = mine
-        for apart, level in ((1, 5), (2, 6), (3, 6)):
-            plane_ref[jnp.bitwise_xor(x, apart) * 4 + at] = jnp.concatenate([units[level][part], blank], axis=0)
-    low_ref[y] = jnp.zeros((PROBES, 128), I16)
-    for apart, level in ((1, 0), (2, 1), (3, 1)):
-        low_ref[jnp.bitwise_xor(y, apart)] = units[level]
+        plane_ref[x * 4 + at] = jnp.concatenate([unit[part] for unit in units[:3]], axis=0)
+        for apart, which in ((1, 3), (2, 4), (3, 4)):
+            plane_ref[jnp.bitwise_xor(x, apart) * 4 + at] = jnp.concatenate([units[which][part], blank], axis=0)
 
 
 def plane_kernel(got_ref, out_ref):
@@ -211,39 +195,58 @@
 
     def total(apart, rows):
         start = jnp.bitwise_xor(x, apart) * 4
-        parts = [decode(got_ref[start + at, rows]) for at in range(4)]
-        return (parts[0] + parts[1]) + (parts[2] + parts[3])
-
-    low, middle, high = slice(0, 16), slice(16, 32), slice(32, 48)
-    sums = [total(0, low), total(0, middle), total(0, high)]
+        return added([decode(got_ref[start + at, rows]) for at in range(4)])
+
+    low = slice(0, QUARTER)
+    chosen = [jnp.zeros((QUARTER, 128), I16)]
+    chosen += [encode(total(0, slice(at * QUARTER, (at + 1) * QUARTER))) for at in range(3)]
     five = encode(total(1, low))
     six = encode(total(2, low) + total(3, low))
-    chosen = [jnp.zeros((QUARTER, 128), I16)] + [encode(value) for value in sums]
     for apart in range(8):
-        which = apart.bit_length()
-        out_ref[jnp.bitwise_xor(z, apart)] = jnp.concatenate([chosen[which], five, six], axis=0)
-
-
-def depth_kernel(got_ref, low_ref, out_ref):
+        piece = jnp.concatenate([chosen[apart.bit_length()], five, six], axis=0)
+        for half in range(2):
+            out_ref[half * 8 + jnp.bitwise_xor(z, apart)] = piece
+
+
+def added(parts):
+    while len(parts) > 1:
+        parts = [a + b for a, b in zip(parts[::2], parts[1::2])]
+    return parts[0]
+
+
+def late_kernel(
+    far_ref, cross_ref, facts_ref, kept_ref, right_ref, got_ref,
+    diagonal_ref, out_ref, sums,
+):
+    y = lax.axis_index("y")
     z = lax.axis_index("z")
-
-    def piece(apart, start):
-        return decode(got_ref[jnp.bitwise_xor(z, apart), start : start + QUARTER])
-
-    two = piece(1, 0)
-    three = piece(2, 0) + piece(3, 0)
-    four = (piece(4, 0) + piece(5, 0)) + (piece(6, 0) + piece(7, 0))
-    found = [two, three, four]
-    for start in (QUARTER, 2 * QUARTER):
-        parts = [piece(apart, start) for apart in range(8)]
-        while len(parts) > 1:
-            parts = [a + b for a, b in zip(parts[::2], parts[1::2])]
-        found.append(parts[0])
-    packed = jnp.concatenate([encode(value) for value in found], axis=0)
-    for at in range(4):
+    sums[...] = kept_ref[...]
+    accumulate(far_ref, facts_ref, right_ref, sums, LATE_SPANS, False)
+    accumulate(cross_ref, facts_ref, right_ref, sums, LATE_SPANS, False)
+    diagonal_ref[...] = sums[:, :, :WIDTH]
+
+    def total(aparts, start):
+        return added([
+            decode(got_ref[half * 8 + jnp.bitwise_xor(z, apart), start : start + QUARTER])
+            for half in range(2) for apart in aparts
+        ])
+
+    found = [
+        total((1,), 0),
+        total((2, 3), 0),
+        total((4, 5, 6, 7), 0),
+        total(range(8), QUARTER),
+        total(range(8), 2 * QUARTER),
+    ]
+    packed = encode(jnp.concatenate(found, axis=0))
+    for core in range(2):
+        out_ref[2 * y + core, 0:PROBES] = jnp.zeros((PROBES, 128), I16)
+    units = [unit_of(sums, level) for level in range(2)]
+    for apart, level in ((1, 0), (2, 1), (3, 1)):
         for core in range(2):
-            out_ref[2 * at + core, 0:PROBES] = low_ref[at]
-            out_ref[2 * at + core, PROBES:] = packed
+            out_ref[2 * jnp.bitwise_xor(y, apart) + core, 0:PROBES] = units[level]
+    for place in range(8):
+        out_ref[place, PROBES:] = packed
 
 
 def final_kernel(got_ref, factor_ref, coupling_ref, diagonal_ref, out_ref, sibling):
@@ -332,56 +335,58 @@
         name="prepare",
     )(*[stay(array) for array in (coords, probes, landmarks, lengthscales)], amplitude)
     far = swap(message, "h")
+    cross = lax.ppermute(message, ("h", "c"), [(0, 3), (1, 2), (2, 1), (3, 0)])
     other = swap(message, "c")
     held, right, factor = pl.pallas_call(
-        near_kernel,
+        own_kernel,
         out_shape=(
             jax.ShapeDtypeStruct((2, PROBES, LANES), F32),
             jax.ShapeDtypeStruct((SPAN, LANES), BF16),
             jax.ShapeDtypeStruct((2, LEVELS * RANK, WIDTH), BF16),
         ),
+        in_specs=[VMEM] * 3,
+        out_specs=(VMEM, VMEM, VMEM),
+        compiler_params=ROOM,
+        cost_estimate=cost(2 * 10**9, 3 * 10**6),
+        name="own",
+    )(message, facts, marks)
+    kept, plane = pl.pallas_call(
+        near_kernel,
+        out_shape=(
+            jax.ShapeDtypeStruct((2, PROBES, KEPT), F32),
+            jax.ShapeDtypeStruct((16, 3 * QUARTER, 128), I16),
+        ),
         in_specs=[VMEM] * 4,
-        out_specs=(VMEM, VMEM, VMEM),
-        compiler_params=ROOM,
-        cost_estimate=cost(2 * 10**9, 3 * 10**6),
+        out_specs=(VMEM, VMEM),
+        scratch_shapes=[pltpu.VMEM((2, PROBES, LANES), F32)],
+        compiler_params=ROOM,
+        cost_estimate=cost(10**9, 2 * 10**6),
         name="near",
-    )(message, other, facts, marks)
-    far, held, right = lax.optimization_barrier((far, held, right))
-    cross = swap(far, "c")
-    diagonal, plane, low = pl.pallas_call(
-        far_kernel,
-        out_shape=(
-            jax.ShapeDtypeStruct((2, PROBES, WIDTH), F32),
-            jax.ShapeDtypeStruct((16, 3 * QUARTER, 128), I16),
-            jax.ShapeDtypeStruct((4, PROBES, 128), I16),
-        ),
-        in_specs=[VMEM] * 5,
-        out_specs=(VMEM, VMEM, VMEM),
-        scratch_shapes=[pltpu.VMEM((2, PROBES, LANES), F32)],
-        compiler_params=ROOM,
-        cost_estimate=cost(10**9, 2 * 10**6),
-        name="far",
-    )(far, cross, facts, held, right)
+    )(other, facts, held, right)
     plane = exchange(plane, ("x", "y"))
     deep = pl.pallas_call(
         plane_kernel,
-        out_shape=jax.ShapeDtypeStruct((8, 3 * QUARTER, 128), I16),
+        out_shape=jax.ShapeDtypeStruct((16, 3 * QUARTER, 128), I16),
         in_specs=[VMEM],
         out_specs=VMEM,
         compiler_params=ROOM,
         cost_estimate=cost(10**5, 3 * 10**5),
         name="plane",
     )(plane)
-    deep = exchange(deep, "z")
-    wide = pl.pallas_call(
-        depth_kernel,
-        out_shape=jax.ShapeDtypeStruct((8, PROBES + 5 * QUARTER, 128), I16),
-        in_specs=[VMEM, VMEM],
-        out_specs=VMEM,
-        compiler_params=ROOM,
-        cost_estimate=cost(10**5, 5 * 10**5),
-        name="depth",
-    )(deep, low)
+    deep = exchange(deep, ("h", "z"))
+    diagonal, wide = pl.pallas_call(
+        late_kernel,
+        out_shape=(
+            jax.ShapeDtypeStruct((2, PROBES, WIDTH), F32),
+            jax.ShapeDtypeStruct((8, PROBES + 5 * QUARTER, 128), I16),
+        ),
+        in_specs=[VMEM] * 6,
+        out_specs=(VMEM, VMEM),
+        scratch_shapes=[pltpu.VMEM((2, PROBES, KEPT), F32)],
+        compiler_params=ROOM,
+        cost_estimate=cost(10**9, 2 * 10**6),
+        name="late",
+    )(far, cross, facts, kept, right, deep)
     wide = exchange(wide, ("y", "c"))
     return pl.pallas_call(
         final_kernel,

time: 81 us -> 85.9 us (1.060)
  blocking collectives: 46.6 us -> 20.7 us
  starting transfers between devices: 21.7 us -> 38 us
  waiting for transfers between devices: 1.93 us -> 16.8 us
    all_to_all x3 -> x2, blocking collectives: 46.6 us -> 20.7 us  [exchange(): return lax.all_to_all(value, axes, 0, 0, tiled=True)]
    all_to_all x0 -> x1, starting transfers between devices: none -> 13.1 us  [exchange(): return lax.all_to_all(value, axes, 0, 0, tiled=True)]
    ppermute x3 -> x2, waiting for transfers between devices: 1.93 us -> 9.64 us  [swap(): return lax.ppermute(value, axis, [(0, 1), (1, 0)])]
    ppermute x0 -> x1, waiting for transfers between devices: none -> 7.15 us  [on_device(): cross = lax.ppermute(message, ('h', 'c'), [(0, 3), (1, 2), (2, 1), (3, 0)])]
    ppermute x0 -> x1, starting transfers between devices: none -> 4.16 us  [on_device(): cross = lax.ppermute(message, ('h', 'c'), [(0, 3), (1, 2), (2, 1), (3, 0)])]
    ppermute x3 -> x2, starting transfers between devices: 21.7 us -> 20.7 us  [swap(): return lax.ppermute(value, axis, [(0, 1), (1, 0)])]
  transfers between devices with their start and end apart: 3 -> 4, of which waited for: 2 -> 2; matrix products, arithmetic and copies ran while one was open for 0% -> 0% of each run, Pallas kernels for 4% -> 2%
where the time goes in v5:
time: 85.9 us; the launch traced here: 85.5 us
  starting transfers between devices  38 us (44%)
  blocking collectives  20.7 us (24%)
  waiting for transfers between devices  16.8 us (20%)
  Pallas kernels  9.38 us (11%)
    ppermute x2, starting transfers between devices, swap(): return lax.ppermute(value, axis, [(0, 1), (1, 0)])  20.7 us
    all_to_all x2, blocking collectives, exchange(): return lax.all_to_all(value, axes, 0, 0, tiled=True)  20.7 us
    all_to_all x1, starting transfers between devices, exchange(): return lax.all_to_all(value, axes, 0, 0, tiled=True)  13.1 us
    ppermute x2, waiting for transfers between devices, swap(): return lax.ppermute(value, axis, [(0, 1), (1, 0)])  9.64 us
    ppermute x1, waiting for transfers between devices, on_device(): cross = lax.ppermute(message, ('h', 'c'), [(0, 3), (1, 2), (2, 1), (3, 0)])  7.15 us
    ppermute x1, starting transfers between devices, on_device(): cross = lax.ppermute(message, ('h', 'c'), [(0, 3), (1, 2), (2, 1), (3, 0)])  4.16 us
    pallas_call x1, Pallas kernels, on_device(): pl.pallas_call(own_kernel, out_shape=(jax.ShapeDtypeStruct((2, PROBES, LA...  2.05 us
    pallas_call x1, Pallas kernels, on_device(): pl.pallas_call(late_kernel, out_shape=(jax.ShapeDtypeStruct((2, PROBES, W...  1.93 us
  transfers between devices with their start and end apart: 4, of which 2 were waited for; matrix products, arithmetic and copies ran while one was open for 0% of the time, Pallas kernels for 2%

profile of v5, /device:TPU:1, one launch (start us, length us, event | category | flops | bytes accessed | tf_op | source)
XLA Modules:
  0.0 85.5 jit_solution(16281725724630873477)
XLA Ops:
  0.7 1.0 %prepare.1 = (bf16[80,512]{1,0:T(8,128)(2,1)S(1)}, f32[7,8,128]{2,1,0:T(8,128)S(1)}, f32[16,128]{1,0:T(8,128)S(1)}) custom-call(s32[8,512]{1,0:T(8,128)} %coords_ref.1, f32[64,512]{1,0:T(8,128)} %probes_ref.1, f32[254,8,128]{2,1,0:T(8,128)} %marks_ref.1, f32[8]{0:T(128)} %scales_ref.1, f32[1]{0:T(128)S(6)} %copy.7.strength_ref), custom_call_target="tpu_custom_call" | custom-call | flops 100000 | bytes 200000 | tf_op jit(solution)/shard_map/prepare/pallas_call | solution.py:318
  1.7 8.7 %collective-permute-start.2 = (bf16[80,512]{1,0:T(8,128)(2,1)S(1)}, bf16[80,512]{1,0:T(8,128)(2,1)S(1)}, u32[]{:S(2)}, u32[]{:S(2)}) collective-permute-start(bf16[80,512]{1,0:T(8,128)(2,1)S(1)} %get-tuple-element.15.own_ref), channel_id=1, source_target_pairs={{0,1},{1,0},{2,3},{3,2},{4,5},{5,4},{6,7},{7,6},{8,9},{9,8},{10,11... | collective-permute-start | bytes 245768 | tf_op jit(solution)/shard_map/ppermute | solution.py:310
  10.4 2.1 %own.1 = (f32[2,64,1024]{2,1,0:T(8,128)S(1)}, bf16[128,1024]{1,0:T(8,128)(2,1)S(1)}, bf16[2,896,512]{2,1,0:T(8,128)(2,1)S(1)}) custom-call(bf16[80,512]{1,0:T(8,128)(2,1)S(1)} %get-tuple-element.15.own_ref, f32[16,128]{1,0:T(8,128)S(1)} %get-tuple-element.16.facts_ref, f32[7,8,128]{2,1,0:T(8,128)S(1)} %get-tuple-element.17.marks_ref), custom_call_target="tpu_custom_call" | custom-call | flops 2000000000 | bytes 3000000 | tf_op jit(solution)/shard_map/own/pallas_call | solution.py:340
  12.5 0.0 collective-permute-done.2.other_ref
  12.5 1.8 %near.1 = (f32[2,64,640]{2,1,0:T(8,128)S(1)}, s16[16,48,128]{2,1,0:T(8,128)(2,1)S(1)}) custom-call(bf16[80,512]{1,0:T(8,128)(2,1)S(1)} %collective-permute-done.2.other_ref, f32[16,128]{1,0:T(8,128)S(1)} %get-tuple-element.16.facts_ref, f32[2,64,1024]{2,1,0:T(8,128)S(1)} %get-tuple-element.18.held_ref, bf16[128,1024]{1,0:T(8,128)(2,1)S(1)} %get-tuple-element.19.right_ref), custom_call_target="tpu_custom_call" | custom-call | flops 1000000000 | bytes 2000000 | tf_op jit(solution)/shard_map/near/pallas_call | solution.py:353
  14.3 10.1 %all_to_all.15.got_ref = s16[16,48,128]{2,1,0:T(8,128)(2,1)S(1)} all-to-all(s16[16,48,128]{2,1,0:T(8,128)(2,1)S(1)} %get-tuple-element.21), channel_id=1, replica_groups=mesh['x'=4,'z'=8,'y'=4,'h'=2,'c'=2] {'x','y'}, dimensions={0} | all-to-all | bytes 393216 | tf_op jit(solution)/shard_map/all_to_all | solution.py:314
  24.4 0.8 plane.1
  25.2 13.1 %all-to-all-start.1 = ((s16[16,48,128]{2,1,0:T(8,128)(2,1)}), s16[16,48,128]{2,1,0:T(8,128)(2,1)S(1)}, u32[]{:S(2)}, u32[]{:S(2)}) async-start(s16[16,48,128]{2,1,0:T(8,128)(2,1)} %plane.1), calls=%async_computation.1 | async-start | bytes 393216 | tf_op jit(solution)/shard_map/all_to_all | solution.py:314
  38.3 12.0 %collective-permute-start = (bf16[80,512]{1,0:T(8,128)(2,1)S(1)}, bf16[80,512]{1,0:T(8,128)(2,1)S(1)}, u32[]{:S(2)}, u32[]{:S(2)}) collective-permute-start(bf16[80,512]{1,0:T(8,128)(2,1)S(1)} %get-tuple-element.15.own_ref), channel_id=1, source_target_pairs={{0,2},{2,0},{1,3},{3,1},{4,6},{6,4},{5,7},{7,5},{8,10},{10,8},{9,1... | collective-permute-start | bytes 245768 | tf_op jit(solution)/shard_map/ppermute | solution.py:310
  50.3 4.2 %collective-permute-start.1 = (bf16[80,512]{1,0:T(8,128)(2,1)S(1)}, bf16[80,512]{1,0:T(8,128)(2,1)S(1)}, u32[]{:S(2)}, u32[]{:S(2)}) collective-permute-start(bf16[80,512]{1,0:T(8,128)(2,1)S(1)} %get-tuple-element.15.own_ref), channel_id=1, source_target_pairs={{0,3},{1,2},{2,1},{3,0},{4,7},{5,6},{6,5},{7,4},{8,11},{9,10},{10,... | collective-permute-start | bytes 245768 | tf_op jit(solution)/shard_map/ppermute | solution.py:338
  54.5 9.6 %collective-permute-done.far_ref = bf16[80,512]{1,0:T(8,128)(2,1)S(1)} collective-permute-done((bf16[80,512]{1,0:T(8,128)(2,1)S(1)}, bf16[80,512]{1,0:T(8,128)(2,1)S(1)}, u32[]{:S(2)}, u32[]{:S(2)}) %collective-permute-start) | collective-permute-done | bytes 81952 | tf_op jit(solution)/shard_map/ppermute | solution.py:310
  64.1 7.2 %collective-permute-done.1.cross_ref = bf16[80,512]{1,0:T(8,128)(2,1)S(1)} collective-permute-done((bf16[80,512]{1,0:T(8,128)(2,1)S(1)}, bf16[80,512]{1,0:T(8,128)(2,1)S(1)}, u32[]{:S(2)}, u32[]{:S(2)}) %collective-permute-start.1) | collective-permute-done | bytes 81952 | tf_op jit(solution)/shard_map/ppermute | solution.py:338
  71.3 0.0 all-to-all-done.1.got_ref
  71.3 0.0 copy-start
  71.3 1.9 %late.1 = (f32[2,64,512]{2,1,0:T(8,128)S(1)}, s16[8,144,128]{2,1,0:T(8,128)(2,1)S(1)}) custom-call(bf16[80,512]{1,0:T(8,128)(2,1)S(1)} %collective-permute-done.far_ref, bf16[80,512]{1,0:T(8,128)(2,1)S(1)} %collective-permute-done.1.cross_ref, f32[16,128]{1,0:T(8,128)S(1)} %get-tuple-element.16.facts_ref, f32[2,64,640]{2,1,0:T(8,128)S(1)} %get-tuple-element.20.kept_ref, ...), custom_call_target="tpu_custom_call" | custom-call | flops 1000000000 | bytes 2000000 | tf_op jit(solution)/shard_map/late/pallas_call | solution.py:377
  73.2 10.6 %all_to_all.16.got_ref = s16[8,144,128]{2,1,0:T(8,128)(2,1)S(1)} all-to-all(s16[8,144,128]{2,1,0:T(8,128)(2,1)S(1)} %get-tuple-element.22), channel_id=1, replica_groups=mesh['x'=4,'z'=8,'y'=4,'h'=2,'c'=2] {'y','c'}, dimensions={0} | all-to-all | bytes 589824 | tf_op jit(solution)/shard_map/all_to_all | solution.py:314
  83.8 0.0 copy-done
  83.8 1.8 %final.1 = f32[2,64,512]{2,1,0:T(8,128)} custom-call(s16[8,144,128]{2,1,0:T(8,128)(2,1)S(1)} %all_to_all.16.got_ref, bf16[2,896,512]{2,1,0:T(8,128)(2,1)S(1)} %get-tuple-element.23.factor_ref, f32[128,128]{1,0:T(8,128)S(1)} %copy-done, f32[2,64,512]{2,1,0:T(8,128)S(1)} %get-tuple-element.24.diagonal_ref), custom_call_target="tpu_custom_call" | custom-call | flops 1000000000 | bytes 3000000 | tf_op jit(solution)/shard_map/final/pallas_call | solution.py:391
Async XLA Ops:
  1.7 10.8 %collective-permute-start.2 = (bf16[80,512]{1,0:T(8,128)(2,1)S(1)}, bf16[80,512]{1,0:T(8,128)(2,1)S(1)}, u32[]{:S(2)}, u32[]{:S(2)}) collective-permute-start(bf16[80,512]{1,0:T(8,128)(2,1)S(1)} %get-tuple-element.15.own_ref), channel_id=1, source_target_pairs={{0,1},{1,0},{2,3},{3,2},{4,5},{5,4},{6,7},{7,6},{8,9},{9,8},{10,11... | collective-permute-start | bytes 245768 | tf_op jit(solution)/shard_map/ppermute | solution.py:310
  25.2 46.0 %all-to-all-start.1 = ((s16[16,48,128]{2,1,0:T(8,128)(2,1)}), s16[16,48,128]{2,1,0:T(8,128)(2,1)S(1)}, u32[]{:S(2)}, u32[]{:S(2)}) async-start(s16[16,48,128]{2,1,0:T(8,128)(2,1)} %plane.1), calls=%async_computation.1 | async-start | bytes 393216 | tf_op jit(solution)/shard_map/all_to_all | solution.py:314
  38.3 25.8 %collective-permute-start = (bf16[80,512]{1,0:T(8,128)(2,1)S(1)}, bf16[80,512]{1,0:T(8,128)(2,1)S(1)}, u32[]{:S(2)}, u32[]{:S(2)}) collective-permute-start(bf16[80,512]{1,0:T(8,128)(2,1)S(1)} %get-tuple-element.15.own_ref), channel_id=1, source_target_pairs={{0,2},{2,0},{1,3},{3,1},{4,6},{6,4},{5,7},{7,5},{8,10},{10,8},{9,1... | collective-permute-start | bytes 245768 | tf_op jit(solution)/shard_map/ppermute | solution.py:310
  50.3 21.0 %collective-permute-start.1 = (bf16[80,512]{1,0:T(8,128)(2,1)S(1)}, bf16[80,512]{1,0:T(8,128)(2,1)S(1)}, u32[]{:S(2)}, u32[]{:S(2)}) collective-permute-start(bf16[80,512]{1,0:T(8,128)(2,1)S(1)} %get-tuple-element.15.own_ref), channel_id=1, source_target_pairs={{0,3},{1,2},{2,1},{3,0},{4,7},{5,6},{6,5},{7,4},{8,11},{9,10},{10,... | collective-permute-start | bytes 245768 | tf_op jit(solution)/shard_map/ppermute | solution.py:338
  71.3 12.5 %copy-start = (f32[128,128]{1,0:T(8,128)S(1)}, f32[128,128]{1,0:T(8,128)}, u32[]{:S(2)}) copy-start(f32[128,128]{1,0:T(8,128)} %coupling_ref.1) | copy-start | bytes 196612

commit v6 on v4

--- a/solution.py
+++ b/solution.py
@@ -34,6 +34,11 @@
     return pl.CostEstimate(flops=flops, bytes_accessed=moved, transcendentals=0)
 
 
+def row_index():
+    z = lax.axis_index("zh") * 2 + lax.axis_index("zl")
+    return lax.axis_index("x") * 32 + z * 4 + lax.axis_index("y")
+
+
 def split3(value):
     first = value.astype(BF16).astype(F32)
     rest = value - first
@@ -99,7 +104,7 @@
     coords_ref, probes_ref, marks_ref, scales_ref, strength_ref,
     out_ref, picked_ref, facts_ref, coords_buf, probes_buf, scales_buf, sem,
 ):
-    row = lax.axis_index("x") * 32 + lax.axis_index("z") * 4 + lax.axis_index("y")
+    row = row_index()
     copies = [
         pltpu.make_async_copy(probes_ref, probes_buf, sem.at[0]),
         pltpu.make_async_copy(coords_ref, coords_buf, sem.at[1]),
@@ -134,14 +139,9 @@
         signs = message[0:PROBES, block * BLOCK : (block + 1) * BLOCK]
         for at in range(0, LANES, BLOCK):
             exponent = jnp.dot(rows, right[:, at : at + BLOCK], preferred_element_type=F32)
-            sums = []
-            for value in kernel_pair(exponent, log_strength):
-                top, rest = halved(value)
-                total = jnp.dot(signs, top, preferred_element_type=F32)
-                if at >= WIDTH:
-                    total = total + jnp.dot(signs, rest, preferred_element_type=F32)
-                sums.append(total)
-            add_k, add_s = sums
+            kern, slope = kernel_pair(exponent, log_strength)
+            add_k = jnp.dot(signs, kern.astype(BF16), preferred_element_type=F32)
+            add_s = jnp.dot(signs, slope.astype(BF16), preferred_element_type=F32)
             if fresh and block == 0:
                 held_k[:, at : at + BLOCK] = add_k
                 held_s[:, at : at + BLOCK] = add_s
@@ -171,76 +171,82 @@
         turned = left_form(marks[level], 0.0).T.astype(BF16)
         exponent = jnp.dot(turned, own_right, preferred_element_type=F32)
         kern, slope = kernel_pair(exponent, log_strength)
-        factor_ref[0, level * RANK : (level + 1) * RANK, :] = kern.astype(BF16)
-        factor_ref[1, level * RANK : (level + 1) * RANK, :] = slope.astype(BF16)
-
-
-def far_kernel(
-    far_ref, cross_ref, facts_ref, held_ref, right_ref,
+        for which, value in enumerate((kern, slope)):
+            top, rest = halved(value)
+            factor_ref[2 * which, level * RANK : (level + 1) * RANK, :] = top
+            factor_ref[2 * which + 1, level * RANK : (level + 1) * RANK, :] = rest
+
+
+def far_kernel(far_ref, facts_ref, held_ref, right_ref, out_ref):
+    inverse = facts_ref[0:8, 0:1]
+    log_strength = facts_ref[8:9, 0:1]
+    out_ref[...] = held_ref[...]
+    accumulate(far_ref, inverse, right_ref[...], log_strength, out_ref.at[0], out_ref.at[1], False)
+
+
+def cross_kernel(
+    cross_ref, facts_ref, held_ref, right_ref,
     diagonal_ref, line_ref, low_ref, sums,
 ):
     y = lax.axis_index("y")
+    zl = lax.axis_index("zl")
     inverse = facts_ref[0:8, 0:1]
     log_strength = facts_ref[8:9, 0:1]
-    right = right_ref[...]
     sums[...] = held_ref[...]
-    accumulate(far_ref, inverse, right, log_strength, sums.at[0], sums.at[1], False)
-    accumulate(cross_ref, inverse, right, log_strength, sums.at[0], sums.at[1], False)
+    accumulate(cross_ref, inverse, right_ref[...], log_strength, sums.at[0], sums.at[1], False)
     diagonal_ref[...] = sums[:, :, :WIDTH]
     units = []
     for level in range(LEVELS):
         at = WIDTH + level * HALF
         pair = [sums[0, :, at : at + HALF], sums[1, :, at : at + HALF]]
         units.append(encode(jnp.concatenate(pair, axis=1)))
+    blank = jnp.zeros((QUARTER, 128), I16)
     for at in range(4):
         part = slice(at * QUARTER, (at + 1) * QUARTER)
-        line_ref[at] = jnp.concatenate([units[level][part] for level in range(2, LEVELS)], axis=0)
+        higher = [units[level][part] for level in range(3, LEVELS)]
+        line_ref[zl * 4 + at] = jnp.concatenate([blank] + higher, axis=0)
+        line_ref[(1 - zl) * 4 + at] = jnp.concatenate([units[2][part]] + higher, axis=0)
     low_ref[y] = jnp.zeros((PROBES, 128), I16)
     for apart, level in ((1, 0), (2, 1), (3, 1)):
         low_ref[jnp.bitwise_xor(y, apart)] = units[level]
 
 
-def line_kernel(got_ref, out_ref):
+def added(parts):
+    while len(parts) > 1:
+        parts = [a + b for a, b in zip(parts[::2], parts[1::2])]
+    return parts[0]
+
+
+def line_kernel(got_ref, out_ref, two_ref):
     x = lax.axis_index("x")
-    z = lax.axis_index("z")
-    total = (decode(got_ref[0]) + decode(got_ref[1])) + (decode(got_ref[2]) + decode(got_ref[3]))
-    packed = encode(total)
-    parts = [packed[at * QUARTER : (at + 1) * QUARTER] for at in range(LEVELS - 2)]
+    zh = lax.axis_index("zh")
+    zl = lax.axis_index("zl")
+    two_ref[...] = encode(added([decode(got_ref[(1 - zl) * 4 + at, 0:QUARTER]) for at in range(4)]))
+    packed = encode(added([decode(got_ref[at, QUARTER:]) for at in range(8)]))
+    parts = [packed[at * QUARTER : (at + 1) * QUARTER] for at in range(4)]
     for aside in range(4):
-        for apart in range(8):
-            place = jnp.bitwise_xor(x, aside) * 8 + jnp.bitwise_xor(z, apart)
+        for apart in range(4):
+            place = jnp.bitwise_xor(x, aside) * 4 + jnp.bitwise_xor(zh, apart)
             if aside > 0:
-                out_ref[place] = parts[2 + aside.bit_length()]
+                out_ref[place] = parts[1 + aside.bit_length()]
             elif apart > 0:
                 out_ref[place] = parts[apart.bit_length() - 1]
             else:
                 out_ref[place] = jnp.zeros((QUARTER, 128), I16)
 
 
-def added(parts):
-    while len(parts) > 1:
-        parts = [a + b for a, b in zip(parts[::2], parts[1::2])]
-    return parts[0]
-
-
-def depth_kernel(got_ref, low_ref, out_ref):
+def depth_kernel(got_ref, two_ref, low_ref, out_ref):
     x = lax.axis_index("x")
-    z = lax.axis_index("z")
+    zh = lax.axis_index("zh")
 
     def total(asides, aparts):
         return added([
-            decode(got_ref[jnp.bitwise_xor(x, aside) * 8 + jnp.bitwise_xor(z, apart)])
+            decode(got_ref[jnp.bitwise_xor(x, aside) * 4 + jnp.bitwise_xor(zh, apart)])
             for aside in asides for apart in aparts
         ])
 
-    found = [
-        total((0,), (1,)),
-        total((0,), (2, 3)),
-        total((0,), (4, 5, 6, 7)),
-        total((1,), range(8)),
-        total((2, 3), range(8)),
-    ]
-    packed = encode(jnp.concatenate(found, axis=0))
+    found = [total((0,), (1,)), total((0,), (2, 3)), total((1,), range(4)), total((2, 3), range(4))]
+    packed = jnp.concatenate([two_ref[...], encode(jnp.concatenate(found, axis=0))], axis=0)
     for at in range(4):
         for core in range(2):
             out_ref[2 * at + core, 0:PROBES] = low_ref[at]
@@ -249,7 +255,7 @@
 
 def final_kernel(got_ref, factor_ref, coupling_ref, diagonal_ref, out_ref, sibling):
     y = lax.axis_index("y")
-    row = lax.axis_index("x") * 32 + lax.axis_index("z") * 4 + y
+    row = row_index()
     for core in range(2):
         lanes = slice(core * 128, core * 128 + 128)
         sibling[0:PROBES, lanes] = decode(got_ref[jnp.bitwise_xor(y, 1) * 2 + core, 0:PROBES])
@@ -293,9 +299,9 @@
     stack = jnp.concatenate([top, rest], axis=0)
     on_kern = jnp.dot(stack, factor_ref[0], preferred_element_type=F32)
     pair = jnp.concatenate([top[:PROBES], rest[:PROBES]], axis=0)
-    on_slope = jnp.dot(pair, factor_ref[1], preferred_element_type=F32)
-    on_kern = on_kern[: 2 * PROBES] + on_kern[2 * PROBES :]
-    on_slope = on_slope[:PROBES] + on_slope[PROBES:]
+    on_slope = jnp.dot(pair, factor_ref[2], preferred_element_type=F32)
+    on_kern = on_kern[: 2 * PROBES] + on_kern[2 * PROBES :] + jnp.dot(top, factor_ref[1], preferred_element_type=F32)
+    on_slope = on_slope[:PROBES] + on_slope[PROBES:] + jnp.dot(top[:PROBES], factor_ref[3], preferred_element_type=F32)
     out_ref[0] = diagonal_ref[0] + on_kern[:PROBES]
     out_ref[1] = diagonal_ref[1] + (on_kern[PROBES:] + on_slope)
 
@@ -339,7 +345,7 @@
         out_shape=(
             jax.ShapeDtypeStruct((2, PROBES, LANES), F32),
             jax.ShapeDtypeStruct((SPAN, LANES), BF16),
-            jax.ShapeDtypeStruct((2, LEVELS * RANK, WIDTH), BF16),
+            jax.ShapeDtypeStruct((4, LEVELS * RANK, WIDTH), BF16),
         ),
         in_specs=[VMEM] * 4,
         out_specs=(VMEM, VMEM, VMEM),
@@ -349,40 +355,52 @@
     )(message, other, facts, marks)
     far, held, right = lax.optimization_barrier((far, held, right))
     cross = swap(far, "c")
+    held = pl.pallas_call(
+        far_kernel,
+        out_shape=jax.ShapeDtypeStruct((2, PROBES, LANES), F32),
+        in_specs=[VMEM] * 4,
+        out_specs=VMEM,
+        compiler_params=ROOM,
+        cost_estimate=cost(10**9, 2 * 10**6),
+        name="far",
+    )(far, facts, held, right)
     diagonal, line, low = pl.pallas_call(
-        far_kernel,
+        cross_kernel,
         out_shape=(
             jax.ShapeDtypeStruct((2, PROBES, WIDTH), F32),
-            jax.ShapeDtypeStruct((4, 5 * QUARTER, 128), I16),
+            jax.ShapeDtypeStruct((8, 5 * QUARTER, 128), I16),
             jax.ShapeDtypeStruct((4, PROBES, 128), I16),
         ),
-        in_specs=[VMEM] * 5,
+        in_specs=[VMEM] * 4,
         out_specs=(VMEM, VMEM, VMEM),
         scratch_shapes=[pltpu.VMEM((2, PROBES, LANES), F32)],
         compiler_params=ROOM,
         cost_estimate=cost(10**9, 2 * 10**6),
-        name="far",
-    )(far, cross, facts, held, right)
-    line = exchange(line, "y")
-    deep = pl.pallas_call(
+        name="cross",
+    )(cross, facts, held, right)
+    line = exchange(line, ("zl", "y"))
+    deep, two = pl.pallas_call(
         line_kernel,
-        out_shape=jax.ShapeDtypeStruct((32, QUARTER, 128), I16),
+        out_shape=(
+            jax.ShapeDtypeStruct((16, QUARTER, 128), I16),
+            jax.ShapeDtypeStruct((QUARTER, 128), I16),
+        ),
         in_specs=[VMEM],
-        out_specs=VMEM,
+        out_specs=(VMEM, VMEM),
         compiler_params=ROOM,
         cost_estimate=cost(10**5, 3 * 10**5),
         name="line",
     )(line)
-    deep = exchange(deep, ("x", "z"))
+    deep = exchange(deep, ("x", "zh"))
     wide = pl.pallas_call(
         depth_kernel,
         out_shape=jax.ShapeDtypeStruct((8, PROBES + 5 * QUARTER, 128), I16),
-        in_specs=[VMEM, VMEM],
+        in_specs=[VMEM] * 3,
         out_specs=VMEM,
         compiler_params=ROOM,
         cost_estimate=cost(10**5, 5 * 10**5),
         name="depth",
-    )(deep, low)
+    )(deep, two, low)
     wide = exchange(wide, ("y", "c"))
     return pl.pallas_call(
         final_kernel,
@@ -397,8 +415,8 @@
 
 
 def solution(mesh):
-    fine = Mesh(mesh.devices.reshape(4, 8, 4, 2, 2), ("x", "z", "y", "h", "c"))
-    every = ("x", "z", "y", "h", "c")
+    fine = Mesh(mesh.devices.reshape(4, 4, 2, 4, 2, 2), ("x", "zh", "zl", "y", "h", "c"))
+    every = ("x", "zh", "zl", "y", "h", "c")
     in_specs = (P(None, every), P(None, every), P(), P(), P(), P())
     return jax.shard_map(
         on_device, mesh=fine, in_specs=in_specs, out_specs=P(None, None, every), check_vma=False

time: 81 us -> 78.9 us (0.974)
  Pallas kernels: 9.72 us -> 7.75 us
    pallas_call x1, Pallas kernels: 3.44 us -> 2.24 us  [on_device(): pl.pallas_call(near_kernel, out_shape=(jax.ShapeDtypeStruct((2, PROBES, L...]
    pallas_call x2 -> x3, Pallas kernels: 3.33 us -> 2.35 us  [the longest x1 1.16 us: on_device(): pl.pallas_call(cross_kernel, out_shape=(jax.ShapeDtypeStruct((2, PROBES,...]
  transfers between devices with their start and end apart: 3 -> 3, of which waited for: 2 -> 1; matrix products, arithmetic and copies ran while one was open for 0% -> 0% of each run, Pallas kernels for 4% -> 4%
where the time goes in v6:
time: 78.9 us; the launch traced here: 78.6 us
  blocking collectives  46.1 us (58%)
  starting transfers between devices  21.8 us (28%)
  Pallas kernels  7.75 us (10%)
  waiting for transfers between devices  2.23 us (3%)
    all_to_all x3, blocking collectives, exchange(): return lax.all_to_all(value, axes, 0, 0, tiled=True)  46.1 us
    ppermute x3, starting transfers between devices, swap(): return lax.ppermute(value, axis, [(0, 1), (1, 0)])  21.8 us
    pallas_call x1, Pallas kernels, on_device(): pl.pallas_call(near_kernel, out_shape=(jax.ShapeDtypeStruct((2, PROBES, L...  2.24 us
    ppermute x3, waiting for transfers between devices, swap(): return lax.ppermute(value, axis, [(0, 1), (1, 0)])  2.23 us
    pallas_call x1, Pallas kernels, on_device(): pl.pallas_call(final_kernel, out_shape=jax.ShapeDtypeStruct((2, PROBES, W...  2.03 us
  transfers between devices with their start and end apart: 3, of which 1 were waited for; matrix products, arithmetic and copies ran while one was open for 0% of the time, Pallas kernels for 4%

profile of v6, /device:TPU:1, one launch (start us, length us, event | category | flops | bytes accessed | tf_op | source)
XLA Modules:
  0.0 78.6 jit_solution(14959692995277778224)
XLA Ops:
  0.7 1.0 %prepare.1 = (bf16[80,512]{1,0:T(8,128)(2,1)S(1)}, f32[7,8,128]{2,1,0:T(8,128)S(1)}, f32[16,128]{1,0:T(8,128)S(1)}) custom-call(s32[8,512]{1,0:T(8,128)} %coords_ref.1, f32[64,512]{1,0:T(8,128)} %probes_ref.1, f32[254,8,128]{2,1,0:T(8,128)} %marks_ref.1, f32[8]{0:T(128)} %scales_ref.1, f32[1]{0:T(128)S(6)} %copy.7.strength_ref), custom_call_target="tpu_custom_call" | custom-call | flops 100000 | bytes 200000 | tf_op jit(solution)/shard_map/prepare/pallas_call | solution.py:322
  1.7 8.7 %collective-permute-start.1 = (bf16[80,512]{1,0:T(8,128)(2,1)S(1)}, bf16[80,512]{1,0:T(8,128)(2,1)S(1)}, u32[]{:S(2)}, u32[]{:S(2)}) collective-permute-start(bf16[80,512]{1,0:T(8,128)(2,1)S(1)} %get-tuple-element.19.own_ref), channel_id=1, source_target_pairs={{0,1},{1,0},{2,3},{3,2},{4,5},{5,4},{6,7},{7,6},{8,9},{9,8},{10,11... | collective-permute-start | bytes 245768 | tf_op jit(solution)/shard_map/ppermute | solution.py:314
  10.4 10.1 %collective-permute-start = (bf16[80,512]{1,0:T(8,128)(2,1)S(1)}, bf16[80,512]{1,0:T(8,128)(2,1)S(1)}, u32[]{:S(2)}, u32[]{:S(2)}) collective-permute-start(bf16[80,512]{1,0:T(8,128)(2,1)S(1)} %get-tuple-element.19.own_ref), channel_id=1, source_target_pairs={{0,2},{2,0},{1,3},{3,1},{4,6},{6,4},{5,7},{7,5},{8,10},{10,8},{9,1... | collective-permute-start | bytes 245768 | tf_op jit(solution)/shard_map/ppermute | solution.py:314
  20.5 0.0 collective-permute-done.1.other_ref
  20.6 2.2 %near.1 = (f32[2,64,1024]{2,1,0:T(8,128)S(1)}, bf16[128,1024]{1,0:T(8,128)(2,1)S(1)}, bf16[4,896,512]{2,1,0:T(8,128)(2,1)S(1)}) custom-call(bf16[80,512]{1,0:T(8,128)(2,1)S(1)} %get-tuple-element.19.own_ref, bf16[80,512]{1,0:T(8,128)(2,1)S(1)} %collective-permute-done.1.other_ref, f32[16,128]{1,0:T(8,128)S(1)} %get-tuple-element.20.facts_ref, ...), custom_call_target="tpu_custom_call" | custom-call | flops 2000000000 | bytes 3000000 | tf_op jit(solution)/shard_map/near/pallas_call | solution.py:343
  22.8 2.2 %collective-permute-done.far_ref = bf16[80,512]{1,0:T(8,128)(2,1)S(1)} collective-permute-done((bf16[80,512]{1,0:T(8,128)(2,1)S(1)}, bf16[80,512]{1,0:T(8,128)(2,1)S(1)}, u32[]{:S(2)}, u32[]{:S(2)}) %collective-permute-start) | collective-permute-done | bytes 81952 | tf_op jit(solution)/shard_map/ppermute | solution.py:314
  25.0 0.0 copy-start
  25.0 3.0 %collective-permute-start.2 = (bf16[80,512]{1,0:T(8,128)(2,1)S(1)}, bf16[80,512]{1,0:T(8,128)(2,1)S(1)}, u32[]{:S(2)}, u32[]{:S(2)}) collective-permute-start(bf16[80,512]{1,0:T(8,128)(2,1)S(1)} %collective-permute-done.far_ref), channel_id=1, source_target_pairs={{0,1},{1,0},{2,3},{3,2},{4,5},{5,4},{6,7},{7,6},{8,9},{9,8},{10,11... | collective-permute-start | bytes 245768 | tf_op jit(solution)/shard_map/ppermute | solution.py:314
  28.0 1.1 %far.1.held_ref = f32[2,64,1024]{2,1,0:T(8,128)S(1)} custom-call(bf16[80,512]{1,0:T(8,128)(2,1)S(1)} %collective-permute-done.far_ref, f32[16,128]{1,0:T(8,128)S(1)} %get-tuple-element.20.facts_ref, f32[2,64,1024]{2,1,0:T(8,128)S(1)} %get-tuple-element.25.held_ref, bf16[128,1024]{1,0:T(8,128)(2,1)S(1)} %get-tuple-element.26.right_ref), custom_call_target="tpu_custom_call" | custom-call | flops 1000000000 | bytes 2000000 | tf_op jit(solution)/shard_map/far/pallas_call | solution.py:358
  29.1 0.0 collective-permute-done.2.cross_ref
  29.1 1.2 %cross.1 = (f32[2,64,512]{2,1,0:T(8,128)S(1)}, s16[8,80,128]{2,1,0:T(8,128)(2,1)S(1)}, s16[4,64,128]{2,1,0:T(8,128)(2,1)S(1)}) custom-call(bf16[80,512]{1,0:T(8,128)(2,1)S(1)} %collective-permute-done.2.cross_ref, f32[16,128]{1,0:T(8,128)S(1)} %get-tuple-element.20.facts_ref, f32[2,64,1024]{2,1,0:T(8,128)S(1)} %far.1.held_ref, ...), custom_call_target="tpu_custom_call" | custom-call | flops 1000000000 | bytes 2000000 | tf_op jit(solution)/shard_map/cross/pallas_call | solution.py:367
  30.3 10.1 %all_to_all.15.got_ref = s16[8,80,128]{2,1,0:T(8,128)(2,1)S(1)} all-to-all(s16[8,80,128]{2,1,0:T(8,128)(2,1)S(1)} %get-tuple-element.27), channel_id=1, replica_groups=mesh['x'=4,'zh'=4,'zl'=2,'y'=4,'h'=2,'c'=2] {'zl','y'}, dimensions={0} | all-to-all | bytes 327680 | tf_op jit(solution)/shard_map/all_to_all | solution.py:318
  40.4 0.1 line.1
  40.5 23.4 %all_to_all.16.got_ref = s16[16,16,128]{2,1,0:T(8,128)(2,1)S(1)} all-to-all(s16[16,16,128]{2,1,0:T(8,128)(2,1)S(1)} %get-tuple-element.28), channel_id=1, replica_groups=mesh['x'=4,'zh'=4,'zl'=2,'y'=4,'h'=2,'c'=2] {'x','zh'}, dimensions={0} | all-to-all | bytes 131072 | tf_op jit(solution)/shard_map/all_to_all | solution.py:318
  63.9 0.1 depth.1
  64.0 12.6 %all_to_all.17.got_ref = s16[8,144,128]{2,1,0:T(8,128)(2,1)S(1)} all-to-all(s16[8,144,128]{2,1,0:T(8,128)(2,1)S(1)} %depth.1), channel_id=1, replica_groups=mesh['x'=4,'zh'=4,'zl'=2,'y'=4,'h'=2,'c'=2] {'y','c'}, dimensions={0} | all-to-all | bytes 589824 | tf_op jit(solution)/shard_map/all_to_all | solution.py:318
  76.6 0.0 copy-done
  76.6 2.0 %final.1 = f32[2,64,512]{2,1,0:T(8,128)} custom-call(s16[8,144,128]{2,1,0:T(8,128)(2,1)S(1)} %all_to_all.17.got_ref, bf16[4,896,512]{2,1,0:T(8,128)(2,1)S(1)} %get-tuple-element.31.factor_ref, f32[128,128]{1,0:T(8,128)S(1)} %copy-done, f32[2,64,512]{2,1,0:T(8,128)S(1)} %get-tuple-element.32.diagonal_ref), custom_call_target="tpu_custom_call" | custom-call | flops 1000000000 | bytes 3000000 | tf_op jit(solution)/shard_map/final/pallas_call | solution.py:405
Async XLA Ops:
  1.7 18.9 %collective-permute-start.1 = (bf16[80,512]{1,0:T(8,128)(2,1)S(1)}, bf16[80,512]{1,0:T(8,128)(2,1)S(1)}, u32[]{:S(2)}, u32[]{:S(2)}) collective-permute-start(bf16[80,512]{1,0:T(8,128)(2,1)S(1)} %get-tuple-element.19.own_ref), channel_id=1, source_target_pairs={{0,1},{1,0},{2,3},{3,2},{4,5},{5,4},{6,7},{7,6},{8,9},{9,8},{10,11... | collective-permute-start | bytes 245768 | tf_op jit(solution)/shard_map/ppermute | solution.py:314
  10.4 14.6 %collective-permute-start = (bf16[80,512]{1,0:T(8,128)(2,1)S(1)}, bf16[80,512]{1,0:T(8,128)(2,1)S(1)}, u32[]{:S(2)}, u32[]{:S(2)}) collective-permute-start(bf16[80,512]{1,0:T(8,128)(2,1)S(1)} %get-tuple-element.19.own_ref), channel_id=1, source_target_pairs={{0,2},{2,0},{1,3},{3,1},{4,6},{6,4},{5,7},{7,5},{8,10},{10,8},{9,1... | collective-permute-start | bytes 245768 | tf_op jit(solution)/shard_map/ppermute | solution.py:314
  25.0 51.5 %copy-start = (f32[128,128]{1,0:T(8,128)S(1)}, f32[128,128]{1,0:T(8,128)}, u32[]{:S(2)}) copy-start(f32[128,128]{1,0:T(8,128)} %coupling_ref.1) | copy-start | bytes 196612
  25.0 4.1 %collective-permute-start.2 = (bf16[80,512]{1,0:T(8,128)(2,1)S(1)}, bf16[80,512]{1,0:T(8,128)(2,1)S(1)}, u32[]{:S(2)}, u32[]{:S(2)}) collective-permute-start(bf16[80,512]{1,0:T(8,128)(2,1)S(1)} %collective-permute-done.far_ref), channel_id=1, source_target_pairs={{0,1},{1,0},{2,3},{3,2},{4,5},{5,4},{6,7},{7,6},{8,9},{9,8},{10,11... | collective-permute-start | bytes 245768 | tf_op jit(solution)/shard_map/ppermute | solution.py:314
